TPU v7x, 32 devices: a whole 2x2x4 slice. The times are simulated.
32 devices in a mesh: pair: 8 (over y, x, core), ga: 4 (over z).
Axes of the slice: x: 2, y: 2, z: 4, core: 2. Of those that a mesh axis runs over, the one named last changes fastest.
Arguments:
- densities: bfloat16 [12288, 4096], P('pair', 'ga'), may hold values from -6 to 6
- val_band: int32 [12288], P('pair'), may hold values from 0 to 127
- cond_band: int32 [12288], P('pair'), may hold values from 0 to 255
- val_energy: float32 [128], replicated, may hold values from -12 to -1
- cond_energy: float32 [256], replicated, may hold values from 1 to 12
Outputs:
- chi: float32 [4096, 4096], P('ga', 'pair')
All inputs are finite; a program needn't handle non-finite values.
Results may differ from a plain program's by a relative error of at most 0.0012.
Values may be sent and summed in bfloat16 or wider, within the bound.
A program may use at most 128 MiB of HBM per device.

v0:
```python
import functools
import math

import jax
import jax.numpy as jnp
from jax import lax
from jax.experimental import pallas as pl
from jax.experimental.pallas import tpu as pltpu
from jax.sharding import PartitionSpec as P

MESH = pl.DeviceIdType.MESH
PLANES, SQUARE = 4, 2
F32, BF16, I16 = jnp.float32, jnp.bfloat16, jnp.int16


def lookup(bands, table):
    levels = lax.broadcasted_iota(jnp.int32, (1, table.shape[0]), 1)
    onehot = (bands[:, None] == levels).astype(jnp.float32)
    return jnp.sum(onehot * table[None, :], axis=1)


def weights(densities, val_band, cond_band, val_energy, cond_energy):
    pairs_total = densities.shape[0] * lax.axis_size("pair")
    gap = lookup(val_band, val_energy) - lookup(cond_band, cond_energy)
    return 4.0 / (gap * math.sqrt(pairs_total))


def scale(weight, block):
    return (weight[:, None] * block.astype(jnp.float32)).astype(jnp.bfloat16)


def contract(left, right):
    return lax.dot_general(
        left, right, (((0,), (0,)), ((), ())), preferred_element_type=jnp.float32
    )


def gather_all(densities, *bands):
    scaled = scale(weights(densities, *bands), densities)
    gathered = lax.all_gather(densities, "ga", axis=1, tiled=True)
    owned = lax.psum_scatter(
        contract(gathered, scaled), "pair", scatter_dimension=0, tiled=True
    )
    return owned.T


STEPS, LOW = 816.0, -27.0


def encode(x):
    t = jnp.log(jnp.abs(x)) * (STEPS / math.log(2)) + (1.5 - LOW * STEPS)
    t = jnp.maximum(t, 0.0).astype(jnp.int32)
    return jnp.where(x < 0, -t, t).astype(I16)


def decode(code):
    c = code.astype(jnp.int32).astype(F32)
    m = jnp.exp2(jnp.abs(c) * (1 / STEPS) + (LOW - 1 / STEPS))
    return jnp.where(c < 0, -m, m)


TILES = (
    (0, 1, 1), (0, 0, 1), (0, 2, 0), (0, 3, 0),
    (2, 1, 0), (2, 0, 0), (3, 1, 0), (3, 0, 0),
    (1, 0, 1), (1, 2, 0), (1, 3, 0),
)
INWARD = ((0, 0), (0, 1), (1, 0), (1, 1), (0, 2), (1, 2), (1, 3), (0, 3))
ARRIVALS = 8
RING = 4


def chunk_slot(block, k, full):
    if block == 0:
        return 0
    if block == 1:
        slots = [INWARD.index((0, k)) + 1]
        if full:
            slots.append(INWARD.index((1, k)) + 1)
        return max(slots)
    return (block - 2) * 4 + k + 1


def piece_slot(tile, k, ch):
    a, b, full = TILES[tile]
    columns = max(chunk_slot(b, 2 * ch, full), chunk_slot(b, 2 * ch + 1, full))
    return max(chunk_slot(a, k, full), columns)


PRIORITY = (6, 7, 4, 5, 10, 9, 8, 3, 0, 2, 1)
PIECES = sorted(
    ((t, k, ch) for t in range(11) for k in range(4) for ch in range(2)),
    key=lambda p: (piece_slot(*p), PRIORITY.index(p[0]), p[1], p[2]),
)
LAST = ARRIVALS + 4


def ranges(slots):
    slots = sorted(slots)
    return [sum(1 for s in slots if s < n) for n in range(LAST + 2)]


def order(items, slot):
    items = sorted(items, key=lambda i: (slot(*i), i))
    return items, ranges([slot(*i) for i in items])


def yd_slot(j, kk):
    return max(piece_slot(4 + j, 2 * v + kk, ch) for v in (0, 1) for ch in (0, 1)) + 1


def xd_slot(t, kk):
    return max(yd_slot(2 * t + x, kk) for x in (0, 1)) + 1


def xt_slot(k):
    return max(piece_slot(j, k, ch) for j in range(4) for ch in (0, 1)) + 1


YD, YD_AT = order([(j, kk) for j in range(4) for kk in range(2)], yd_slot)
XD, XD_AT = order([(t, kk) for t in range(2) for kk in range(2)], xd_slot)
PIECE_AT = ranges([piece_slot(*p) for p in PIECES])
G_ORDER = []
for p in PIECES:
    if p[0] >= 8 and (p[0] - 7, p[1]) not in G_ORDER:
        G_ORDER.append((p[0] - 7, p[1]))


def pick(index, values):
    result = jnp.int32(values[0])
    for n, value in enumerate(values):
        if n and value != values[0]:
            result = jnp.where(index == n, value, result)
    return result


def many(start, stop, body):
    def step(n, carry):
        body(n)
        return carry

    lax.fori_loop(start, stop, step, 0)


def kernel(
    dens, weight, out, mb, st, drecv, dsend, acc, keep, keepd, xr, yr, yrd, xrd, din, dfw,
    load_sem, in_s, in_r, mid_s, mid_r, p_s, p_r, xt_s, xt_r, yt_s, yt_r,
    yd_s, yd_r, xd_s, xd_r, zd_s, zd_r, fw_s, fw_r, g_s, g_r,
):
    pair, z = lax.axis_index("pair"), lax.axis_index("ga")
    c = pair % 2
    x = (pair // 2) % 2
    y = pair // 4
    h = z // 2
    X = (x + h) % 2
    Y = (y + h) % 2
    inner = (z == 1) | (z == 2)
    outer = (z == 0) | (z == 3)

    pairs, width = dens.shape
    half = pairs // 2
    rb = width // 4
    hw = width // 2
    kb = 256 if half % 256 == 0 else half
    keep_off = h * half
    give_off = (1 - h) * half

    def at(yy, xx, cc, zz):
        return ((yy * SQUARE + xx) * 2 + cc, zz)

    to_core = at(y, x, 1 - c, z)
    to_x = at(y, 1 - x, c, z)
    to_y = at(1 - y, x, c, z)
    z_mate = z + 1 - 2 * (z % 2)
    z_cross = 3 - z
    to_mate = at(y, x, c, z_mate)
    to_cross = at(y, x, c, z_cross)

    def remote(src, dst, send, recv, to):
        return pltpu.make_async_remote_copy(
            src_ref=src, dst_ref=dst, send_sem=send, recv_sem=recv,
            device_id=to, device_id_type=MESH,
        )

    def rows(k, size=rb):
        return pl.ds(pl.multiple_of(k * size, size), size)

    def part(off):
        return pl.ds(pl.multiple_of(off, half), half)

    def columns(k):
        return pl.ds(pl.multiple_of(k * rb, rb), rb)

    def sides(k):
        return pl.ds(pl.multiple_of(k * hw, hw), hw)

    barrier = pltpu.get_barrier_semaphore()
    for to in (to_core, to_x, to_y, to_mate):
        pl.semaphore_signal(barrier, inc=1, device_id=to, device_id_type=MESH)

    @pl.when(inner)
    def _():
        pl.semaphore_signal(barrier, inc=1, device_id=to_cross, device_id_type=MESH)
        pl.semaphore_wait(barrier, 5)

    @pl.when(outer)
    def _():
        pl.semaphore_wait(barrier, 4)

    def inward(n):
        kind = pick(n, [i[0] for i in INWARD])
        k = pick(n, [i[1] for i in INWARD])
        off = jnp.where(kind == 0, keep_off, give_off)
        return remote(
            dens.at[part(off), columns(k)], mb.at[1, part(off), columns(k)],
            in_s.at[n], in_r.at[n], to_mate,
        ), kind, k, off

    def across(k):
        return remote(
            dens.at[part(give_off), columns(k)], mb.at[2, part(give_off), columns(k)],
            mid_s.at[k], mid_r.at[k], to_cross,
        )

    def relay(k):
        return remote(
            mb.at[1, part(give_off), columns(k)], mb.at[3, part(give_off), columns(k)],
            mid_s.at[4 + k], mid_r.at[4 + k], to_cross,
        )

    def middle_in(n):
        block, k = 2 + n // 4, n % 4
        return remote(
            mb.at[block, part(keep_off), columns(k)], mb.at[block, part(keep_off), columns(k)],
            mid_s.at[n], mid_r.at[n], to_cross,
        ), block, k

    def swap(slot, tile, k):
        return remote(
            dsend.at[slot], drecv.at[tile, rows(k)],
            p_s.at[slot], p_r.at[tile * 4 + k], to_core,
        )

    def xt(g, k, j):
        return remote(
            drecv.at[j, rows(k)], xr.at[g, rows(k)], xt_s.at[g * 4 + k], xt_r.at[g * 4 + k], to_x
        )

    def yt(k):
        return remote(xr.at[1 - Y, rows(k)], yr.at[rows(k)], yt_s.at[k], yt_r.at[k], to_y)

    def yd(j, kk):
        return remote(
            drecv.at[4 + j, rows(2 * Y + kk)], yrd.at[j, rows(kk)],
            yd_s.at[j * 2 + kk], yd_r.at[j * 2 + kk], to_y,
        )

    def xd(t, kk, j):
        return remote(
            yrd.at[j, rows(kk)], xrd.at[t, rows(kk)],
            xd_s.at[t * 2 + kk], xd_r.at[t * 2 + kk], to_x,
        )

    def zd(t, kk):
        return remote(
            xrd.at[t, rows(kk)], din.at[t, rows(kk)],
            zd_s.at[t * 2 + kk], zd_r.at[t * 2 + kk], to_cross,
        )

    def forward(kk):
        return remote(din.at[1, rows(kk)], din.at[0, rows(kk)], fw_s.at[kk], fw_r.at[kk], to_mate)

    def grow(j, k):
        n = (j - 1) * 4 + k
        return remote(
            drecv.at[7 + j, rows(k)], drecv.at[j, rows(k)], g_s.at[n], g_r.at[n], to_mate
        )

    def transpose(block, off, k):
        def step(n):
            r = pl.ds(pl.multiple_of(off + n * kb, kb), kb)
            t = mb[block, r, columns(k)].T
            st[block, columns(k), r] = (t.astype(F32) * weight[:, r]).astype(BF16)

        many(0, half // kb, step)

    def product(a, b, full, k, ch):
        acc[...] = jnp.dot(
            st[a, rows(k), part(keep_off)], mb[b, part(keep_off), sides(ch)],
            preferred_element_type=F32,
        )

        @pl.when(full == 1)
        def _():
            acc[...] += jnp.dot(
                st[a, rows(k), part(give_off)], mb[b, part(give_off), sides(ch)],
                preferred_element_type=F32,
            )

    def kept(j, k, value):
        keep[j // 2, rows(k)] = value

    load = pltpu.make_async_copy(dens, mb.at[0], load_sem)

    @pl.when(outer)
    def _():
        many(0, ARRIVALS, lambda n: inward(n)[0].start())

    @pl.when(inner)
    def _():
        many(0, 4, lambda k: across(k).start())

    load.start()
    load.wait()

    def own(k):
        transpose(0, keep_off, k)
        transpose(0, give_off, k)

    many(0, 4, own)

    def give_away(k, j, value):
        drecv[j, rows(k)] = encode(value)

    def settle(tile, k):
        swap(0, tile, k).wait_recv()
        value = acc[...] + decode(drecv[tile, rows(k)])

        @pl.when(tile < 4)
        def _():
            @pl.when(tile % 2 == X)
            def _():
                kept(tile, k, value)

            @pl.when(tile % 2 != X)
            def _():
                drecv[tile, rows(k)] = encode(value)
                xt(tile // 2, k, tile).start()

        @pl.when((tile >= 4) & (tile < 8))
        def _():
            @pl.when(k // 2 == Y)
            def _():
                drecv[tile, rows(k)] = encode(value)
                yd(tile - 4, k % 2).start()

            @pl.when(k // 2 != Y)
            def _():
                keepd[tile - 4, rows(k % 2)] = value

        @pl.when(tile >= 8)
        def _():
            drecv[tile, rows(k)] = encode(value)
            grow(tile - 7, k).start()

    def send_part(n, tile, k):
        slot = n % RING

        @pl.when(n >= RING)
        def _():
            swap(slot, tile, k).wait_send()

        dsend[slot] = encode(acc[...])
        swap(slot, tile, k).start()

    def finish_ring():
        many(0, RING, lambda n: swap(n, 0, 0).wait_send())

    def give_y(k):
        xt(1 - Y, k, 0).wait_recv()
        value = keep[1 - Y, rows(k)] + decode(xr[1 - Y, rows(k)])
        late = (Y == 0) & (k // 2 == 0)

        @pl.when(late)
        def _():
            xr[1 - Y, rows(k)] = encode(value + decode(din[0, rows(k % 2)]))

        @pl.when(late == False)
        def _():
            xr[1 - Y, rows(k)] = encode(value)

        yt(k).start()

    def finish(k):
        xt(Y, k, 0).wait_recv()
        yt(k).wait_recv()
        value = keep[Y, rows(k)] + decode(xr[Y, rows(k)]) + decode(yr[rows(k)])
        late = (Y == 1) & (k // 2 == 1)

        @pl.when(late)
        def _():
            out[rows(k)] = value + decode(din[0, rows(k % 2)])

        @pl.when(late == False)
        def _():
            out[rows(k)] = value

    def last_stages(wait_din):
        many(0, 2, lambda n: give_y(2 * (1 - Y) * (1 - Y) + 2 * Y * (1 - Y) + n))
        wait_din()
        many(0, 2, lambda n: give_y(2 * Y + n))
        many(0, 4, finish)

    def wait_sends():
        def step(k):
            xt(0, k, 0).wait_send()
            xt(1, k, 0).wait_send()
            yt(k).wait_send()

        many(0, 4, step)

    @pl.when(inner)
    def _():
        def slot_step(s):
            @pl.when((s >= 1) & (s <= ARRIVALS))
            def _():
                n = s - 1
                copy, block, k = middle_in(n)
                copy.wait_recv()
                transpose(block, keep_off, k)
                copy, kind, k, off = inward(n)
                copy.wait_recv()

                @pl.when(kind == 1)
                def _():
                    relay(k).start()

                transpose(1, off, k)

            first, last = pick(s, PIECE_AT), pick(s + 1, PIECE_AT)

            def at_piece(n):
                tile = pick(n, [p[0] for p in PIECES])
                k = pick(n, [p[1] for p in PIECES])
                ch = pick(n, [p[2] for p in PIECES])
                a = pick(tile, [t[0] for t in TILES])
                b = pick(tile, [t[1] for t in TILES])
                full = pick(tile, [t[2] for t in TILES])
                return tile, k, ch, a, b, full

            def other(n, sent):
                tile, k, ch, a, b, full = at_piece(n)

                @pl.when(ch != c)
                def _():
                    product(a, b, full, k, ch)
                    send_part(sent, tile, k)

                return sent + jnp.where(ch != c, 1, 0)

            def mine(n):
                tile, k, ch, a, b, full = at_piece(n)

                @pl.when(ch == c)
                def _():
                    product(a, b, full, k, ch)
                    settle(tile, k)

            def before(n):
                total = jnp.int32(0)
                for m, p in enumerate(PIECES):
                    total = total + jnp.where((m < n) & (p[2] != c), 1, 0)
                return total

            lax.fori_loop(first, last, other, before(first))
            many(first, last, mine)

            def yd_in(n):
                j = pick(n, [i[0] for i in YD])
                kk = pick(n, [i[1] for i in YD])
                yd(j, kk).wait_recv()
                value = keepd[j, rows(kk)] + decode(yrd[j, rows(kk)])

                @pl.when(j % 2 == X)
                def _():
                    keepd[j, rows(kk)] = value

                @pl.when(j % 2 != X)
                def _():
                    yrd[j, rows(kk)] = encode(value)
                    xd(j // 2, kk, j).start()

            many(pick(s, YD_AT), pick(s + 1, YD_AT), yd_in)

            def xd_in(n):
                t = pick(n, [i[0] for i in XD])
                kk = pick(n, [i[1] for i in XD])
                xd(t, kk, 0).wait_recv()
                value = keepd[2 * t + X, rows(kk)] + decode(xrd[t, rows(kk)])
                xrd[t, rows(kk)] = encode(value)
                zd(t, kk).start()

            many(pick(s, XD_AT), pick(s + 1, XD_AT), xd_in)

        many(0, LAST + 1, slot_step)

        def pass_on(kk):
            zd(1, kk).wait_recv()
            forward(kk).start()

        def wait_din():
            many(0, 2, pass_on)
            many(0, 2, lambda kk: zd(0, kk).wait_recv())

        last_stages(wait_din)
        finish_ring()
        wait_sends()

        def ends(n):
            middle_in(n)[0].wait_send()
            yd(n // 2, n % 2).wait_send()

        many(0, 8, ends)

        def ends4(n):
            xd(n // 2, n % 2, 0).wait_send()
            zd(n // 2, n % 2).wait_send()

        many(0, 4, ends4)
        many(0, 2, lambda kk: forward(kk).wait_send())
        many(0, 12, lambda n: grow(1 + n // 4, n % 4).wait_send())

    @pl.when(outer)
    def _():
        def other(k):
            product(0, 0, jnp.int32(1), k, 1 - c)
            send_part(k, jnp.int32(0), k)

        def mine(k):
            product(0, 0, jnp.int32(1), k, c)
            settle(jnp.int32(0), k)

        many(0, 4, other)
        many(0, 4, mine)

        def arrived(n):
            j = pick(n, [i[0] for i in G_ORDER])
            k = pick(n, [i[1] for i in G_ORDER])
            grow(j, k).wait_recv()

            @pl.when(j % 2 == X)
            def _():
                kept(j, k, decode(drecv[j, rows(k)]))

            @pl.when(j % 2 != X)
            def _():
                xt(j // 2, k, j).start()

        many(0, 12, arrived)
        last_stages(lambda: many(0, 2, lambda kk: forward(kk).wait_recv()))
        finish_ring()
        wait_sends()
        many(0, ARRIVALS, lambda n: inward(n)[0].wait_send())


def one_kernel(densities, *bands):
    weight = weights(densities, *bands)[None, :]
    pairs, width = densities.shape
    rb, hw = width // 4, width // 2
    dma = pltpu.SemaphoreType.DMA
    counts = (8, 8, 8, 8, RING, 44, 8, 8, 4, 4, 8, 8, 4, 4, 4, 4, 2, 2, 12, 12)
    return pl.pallas_call(
        kernel,
        out_shape=jax.ShapeDtypeStruct((width, hw), F32),
        in_specs=[
            pl.BlockSpec(memory_space=pl.ANY),
            pl.BlockSpec(memory_space=pltpu.VMEM),
        ],
        out_specs=pl.BlockSpec(memory_space=pltpu.VMEM),
        scratch_shapes=[
            pltpu.VMEM((4, pairs, width), BF16),
            pltpu.VMEM((4, width, pairs), BF16),
            pltpu.VMEM((11, width, hw), I16),
            pltpu.VMEM((RING, rb, hw), I16),
            pltpu.VMEM((rb, hw), F32),
            pltpu.VMEM((2, width, hw), F32),
            pltpu.VMEM((4, hw, hw), F32),
            pltpu.VMEM((2, width, hw), I16),
            pltpu.VMEM((width, hw), I16),
            pltpu.VMEM((4, hw, hw), I16),
            pltpu.VMEM((2, hw, hw), I16),
            pltpu.VMEM((2, hw, hw), I16),
            pltpu.VMEM((8, 128), I16),
            dma,
        ]
        + [dma((n,)) for n in counts],
        compiler_params=pltpu.CompilerParams(
            collective_id=0, has_side_effects=True, vmem_limit_bytes=62 * 2**20
        ),
    )(densities, weight)


def solution(mesh):
    placed = (P("pair", "ga"), P("pair"), P("pair"), P(), P())
    square = mesh.shape["ga"] == PLANES and mesh.shape["pair"] == 2 * SQUARE**2
    return jax.shard_map(
        one_kernel if square else gather_all,
        mesh=mesh,
        in_specs=placed,
        out_specs=P("ga", "pair"),
        check_vma=False,
    )
```

profile of v0, /device:TPU:7, one launch (start us, length us, event | category | flops | bytes accessed | tf_op | source)
XLA Modules:
  0.0 177.2 jit_solution(4773308726783594826)
XLA Ops:
  0.0 1.2 select_reduce_fusion.1
  1.2 1.2 select_reduce_fusion
  2.4 0.6 div.18.weight
  3.0 171.1 %shard_map.55 = f32[1024,512]{1,0:T(8,128)} custom-call(bf16[1536,1024]{1,0:T(8,128)(2,1)} %dens.1, f32[1,1536]{1,0:T(1,128)} %div.18.weight), custom_call_target="tpu_custom_call" | custom-call | tf_op jit(solution)/shard_map/pallas_call | solution.py:561
  174.1 3.1 %copy.7 = f32[1024,512]{1,0:T(8,128)} copy(f32[1024,512]{1,0:T(8,128)} %shard_map.55) | data formatting | bytes 4194304
  (1 shorter events, 0.0 us)
where the time goes:
time: 178 us; the launch traced here: 177 us
  Pallas kernels  171 us (96%)
  local copies, waits for them, and re-layouts  3.68 us (2%)
  other arithmetic  2.43 us (1%)
    pallas_call x1, Pallas kernels, one_kernel(): pl.pallas_call(kernel, out_shape=jax.ShapeDtypeStruct((width, hw), F32),...  171 us

commit v1 on v0

--- a/solution.py
+++ b/solution.py
@@ -48,13 +48,12 @@
 
 
 def encode(x):
-    t = jnp.log(jnp.abs(x)) * (STEPS / math.log(2)) + (1.5 - LOW * STEPS)
-    t = jnp.maximum(t, 0.0).astype(jnp.int32)
-    return jnp.where(x < 0, -t, t).astype(I16)
+    t = jnp.maximum(jnp.log2(jnp.abs(x)) * STEPS + (1.5 - LOW * STEPS), 0.0)
+    return jnp.where(x < 0, -t, t).astype(jnp.int32).astype(I16)
 
 
 def decode(code):
-    c = code.astype(jnp.int32).astype(F32)
+    c = code.astype(F32)
     m = jnp.exp2(jnp.abs(c) * (1 / STEPS) + (LOW - 1 / STEPS))
     return jnp.where(c < 0, -m, m)
 
@@ -64,9 +63,9 @@
     (2, 1, 0), (2, 0, 0), (3, 1, 0), (3, 0, 0),
     (1, 0, 1), (1, 2, 0), (1, 3, 0),
 )
-INWARD = ((0, 0), (0, 1), (1, 0), (1, 1), (0, 2), (1, 2), (1, 3), (0, 3))
+INWARD = ((0, 0), (0, 1), (1, 0), (1, 1), (1, 2), (1, 3), (0, 2), (0, 3))
 ARRIVALS = 8
-RING = 4
+RING, SENDS, LAG = 8, 4, 2
 
 
 def chunk_slot(block, k, full):
@@ -83,14 +82,21 @@
 def piece_slot(tile, k, ch):
     a, b, full = TILES[tile]
     columns = max(chunk_slot(b, 2 * ch, full), chunk_slot(b, 2 * ch + 1, full))
-    return max(chunk_slot(a, k, full), columns)
+    slot = max(chunk_slot(a, k, full), columns)
+    if slot == ARRIVALS and not 4 <= tile < 8:
+        slot += 1 if tile >= 8 else 2
+    return slot
 
 
 PRIORITY = (6, 7, 4, 5, 10, 9, 8, 3, 0, 2, 1)
-PIECES = sorted(
-    ((t, k, ch) for t in range(11) for k in range(4) for ch in range(2)),
-    key=lambda p: (piece_slot(*p), PRIORITY.index(p[0]), p[1], p[2]),
-)
+PIECES = [
+    sorted(
+        ((t, k) for t in range(11) for k in range(4)),
+        key=lambda p: (piece_slot(*p, ch), PRIORITY.index(p[0]), p[1]),
+    )
+    for ch in range(2)
+]
+COUNT = 44
 LAST = ARRIVALS + 4
 
 
@@ -104,25 +110,23 @@
     return items, ranges([slot(*i) for i in items])
 
 
-def yd_slot(j, kk):
-    return max(piece_slot(4 + j, 2 * v + kk, ch) for v in (0, 1) for ch in (0, 1)) + 1
-
-
-def xd_slot(t, kk):
-    return max(yd_slot(2 * t + x, kk) for x in (0, 1)) + 1
-
-
-def xt_slot(k):
-    return max(piece_slot(j, k, ch) for j in range(4) for ch in (0, 1)) + 1
-
-
-YD, YD_AT = order([(j, kk) for j in range(4) for kk in range(2)], yd_slot)
-XD, XD_AT = order([(t, kk) for t in range(2) for kk in range(2)], xd_slot)
-PIECE_AT = ranges([piece_slot(*p) for p in PIECES])
-G_ORDER = []
-for p in PIECES:
-    if p[0] >= 8 and (p[0] - 7, p[1]) not in G_ORDER:
-        G_ORDER.append((p[0] - 7, p[1]))
+def yd_slot(ch, j, kk):
+    return max(piece_slot(4 + j, 2 * v + kk, ch) for v in (0, 1)) + 1
+
+
+def xd_slot(ch, t, kk):
+    return max(ARRIVALS, *(yd_slot(ch, 2 * t + x, kk) for x in (0, 1))) + 1
+
+
+def both(items, slot):
+    found = [order(items, functools.partial(slot, ch)) for ch in range(2)]
+    return [f[0] for f in found], [f[1] for f in found]
+
+
+YD, YD_AT = both([(j, kk) for j in range(4) for kk in range(2)], yd_slot)
+XD, XD_AT = both([(t, kk) for t in range(2) for kk in range(2)], xd_slot)
+PIECE_AT = [ranges([piece_slot(*p, ch) for p in PIECES[ch]]) for ch in range(2)]
+G_ORDER = [[(t - 7, k) for t, k in PIECES[ch] if t >= 8] for ch in range(2)]
 
 
 def pick(index, values):
@@ -133,6 +137,23 @@
     return result
 
 
+def pick2(side, index, values):
+    return jnp.where(side == 0, pick(index, values[0]), pick(index, values[1]))
+
+
+def packed(side, index, codes):
+    words = [
+        [sum(v << (6 * i) for i, v in enumerate(c[n : n + 5])) for n in range(0, len(c), 5)]
+        for c in codes
+    ]
+    word, place = pick2(side, lax.div(index, 5), words), lax.rem(index, 5)
+    result = lax.rem(word, 64)
+    for i in range(1, 5):
+        word = lax.div(word, 64)
+        result = jnp.where(place == i, lax.rem(word, 64), result)
+    return result
+
+
 def many(start, stop, body):
     def step(n, carry):
         body(n)
@@ -142,9 +163,9 @@
 
 
 def kernel(
-    dens, weight, out, mb, st, drecv, dsend, acc, keep, keepd, xr, yr, yrd, xrd, din, dfw,
-    load_sem, in_s, in_r, mid_s, mid_r, p_s, p_r, xt_s, xt_r, yt_s, yt_r,
-    yd_s, yd_r, xd_s, xd_r, zd_s, zd_r, fw_s, fw_r, g_s, g_r,
+    dens, weight, out, mb, st, drecv, dsend, ring, acc, keep, keepd, keepg, xr, yr, yrd, xrd, din,
+    load_sem, credit, in_s, in_r, mid_s, mid_r, p_s, p_r, xt_s, xt_r, yt_s, yt_r,
+    yd_s, yd_r, xd_s, xd_r, zd_s, zd_r, g_s, g_r,
 ):
     pair, z = lax.axis_index("pair"), lax.axis_index("ga")
     c = pair % 2
@@ -234,10 +255,9 @@
             mid_s.at[n], mid_r.at[n], to_cross,
         ), block, k
 
-    def swap(slot, tile, k):
-        return remote(
-            dsend.at[slot], drecv.at[tile, rows(k)],
-            p_s.at[slot], p_r.at[tile * 4 + k], to_core,
+    def swap(n):
+        return remote(
+            dsend.at[n % SENDS], ring.at[n % RING], p_s.at[n % SENDS], p_r.at[n % RING], to_core
         )
 
     def xt(g, k, j):
@@ -265,9 +285,6 @@
             xrd.at[t, rows(kk)], din.at[t, rows(kk)],
             zd_s.at[t * 2 + kk], zd_r.at[t * 2 + kk], to_cross,
         )
-
-    def forward(kk):
-        return remote(din.at[1, rows(kk)], din.at[0, rows(kk)], fw_s.at[kk], fw_r.at[kk], to_mate)
 
     def grow(j, k):
         n = (j - 1) * 4 + k
@@ -283,18 +300,17 @@
 
         many(0, half // kb, step)
 
-    def product(a, b, full, k, ch):
-        acc[...] = jnp.dot(
-            st[a, rows(k), part(keep_off)], mb[b, part(keep_off), sides(ch)],
-            preferred_element_type=F32,
-        )
+    def product(a, b, full, k, ch, put):
+        @pl.when(full == 0)
+        def _():
+            put(jnp.dot(
+                st[a, rows(k), part(keep_off)], mb[b, part(keep_off), sides(ch)],
+                preferred_element_type=F32,
+            ))
 
         @pl.when(full == 1)
         def _():
-            acc[...] += jnp.dot(
-                st[a, rows(k), part(give_off)], mb[b, part(give_off), sides(ch)],
-                preferred_element_type=F32,
-            )
+            put(jnp.dot(st[a, rows(k)], mb[b, :, sides(ch)], preferred_element_type=F32))
 
     def kept(j, k, value):
         keep[j // 2, rows(k)] = value
@@ -318,63 +334,78 @@
 
     many(0, 4, own)
 
-    def give_away(k, j, value):
-        drecv[j, rows(k)] = encode(value)
-
-    def settle(tile, k):
-        swap(0, tile, k).wait_recv()
-        value = acc[...] + decode(drecv[tile, rows(k)])
-
-        @pl.when(tile < 4)
-        def _():
-            @pl.when(tile % 2 == X)
+    def theirs(n, a, b, full, k):
+        @pl.when(n >= SENDS)
+        def _():
+            swap(n).wait_send()
+
+        @pl.when(n >= RING)
+        def _():
+            pl.semaphore_wait(credit, 1)
+
+        def put(value):
+            dsend[n % SENDS] = value
+
+        product(a, b, full, k, 1 - c, put)
+        swap(n).start()
+
+    def settle(n, count, tile, a, b, full, k):
+        swap(n).wait_recv()
+
+        def put(value):
+            acc[...] = value + ring[n % RING]
+
+        product(a, b, full, k, c, put)
+
+        @pl.when(n < count - RING)
+        def _():
+            pl.semaphore_signal(credit, inc=1, device_id=to_core, device_id_type=MESH)
+
+        @pl.when((tile < 4) & (tile % 2 == X))
+        def _():
+            kept(tile, k, acc[...])
+
+        stays = (tile >= 4) & (tile < 8) & (k // 2 != Y)
+
+        @pl.when(stays)
+        def _():
+            keepd[tile - 4, rows(k % 2)] = acc[...]
+
+        later = (tile == 9 + X) & (k // 2 == Y)
+
+        @pl.when(later)
+        def _():
+            keepg[rows(k % 2)] = acc[...]
+
+        @pl.when(jnp.logical_not(stays | later | ((tile < 4) & (tile % 2 == X))))
+        def _():
+            drecv[tile, rows(k)] = encode(acc[...])
+
+            @pl.when(tile < 4)
             def _():
-                kept(tile, k, value)
-
-            @pl.when(tile % 2 != X)
+                xt(tile // 2, k, tile).start()
+
+            @pl.when((tile >= 4) & (tile < 8))
             def _():
-                drecv[tile, rows(k)] = encode(value)
-                xt(tile // 2, k, tile).start()
-
-        @pl.when((tile >= 4) & (tile < 8))
-        def _():
-            @pl.when(k // 2 == Y)
+                yd(tile - 4, k % 2).start()
+
+            @pl.when(tile >= 8)
             def _():
-                drecv[tile, rows(k)] = encode(value)
-                yd(tile - 4, k % 2).start()
-
-            @pl.when(k // 2 != Y)
-            def _():
-                keepd[tile - 4, rows(k % 2)] = value
-
-        @pl.when(tile >= 8)
-        def _():
-            drecv[tile, rows(k)] = encode(value)
-            grow(tile - 7, k).start()
-
-    def send_part(n, tile, k):
-        slot = n % RING
-
-        @pl.when(n >= RING)
-        def _():
-            swap(slot, tile, k).wait_send()
-
-        dsend[slot] = encode(acc[...])
-        swap(slot, tile, k).start()
+                grow(tile - 7, k).start()
 
     def finish_ring():
-        many(0, RING, lambda n: swap(n, 0, 0).wait_send())
+        many(0, SENDS, lambda n: swap(n).wait_send())
 
     def give_y(k):
         xt(1 - Y, k, 0).wait_recv()
         value = keep[1 - Y, rows(k)] + decode(xr[1 - Y, rows(k)])
-        late = (Y == 0) & (k // 2 == 0)
+        late = inner & (Y == 0) & (k // 2 == 0)
 
         @pl.when(late)
         def _():
             xr[1 - Y, rows(k)] = encode(value + decode(din[0, rows(k % 2)]))
 
-        @pl.when(late == False)
+        @pl.when(jnp.logical_not(late))
         def _():
             xr[1 - Y, rows(k)] = encode(value)
 
@@ -384,13 +415,13 @@
         xt(Y, k, 0).wait_recv()
         yt(k).wait_recv()
         value = keep[Y, rows(k)] + decode(xr[Y, rows(k)]) + decode(yr[rows(k)])
-        late = (Y == 1) & (k // 2 == 1)
+        late = inner & (Y == 1) & (k // 2 == 1)
 
         @pl.when(late)
         def _():
             out[rows(k)] = value + decode(din[0, rows(k % 2)])
 
-        @pl.when(late == False)
+        @pl.when(jnp.logical_not(late))
         def _():
             out[rows(k)] = value
 
@@ -426,47 +457,31 @@
 
                 transpose(1, off, k)
 
-            first, last = pick(s, PIECE_AT), pick(s + 1, PIECE_AT)
-
-            def at_piece(n):
-                tile = pick(n, [p[0] for p in PIECES])
-                k = pick(n, [p[1] for p in PIECES])
-                ch = pick(n, [p[2] for p in PIECES])
-                a = pick(tile, [t[0] for t in TILES])
-                b = pick(tile, [t[1] for t in TILES])
-                full = pick(tile, [t[2] for t in TILES])
-                return tile, k, ch, a, b, full
-
-            def other(n, sent):
-                tile, k, ch, a, b, full = at_piece(n)
-
-                @pl.when(ch != c)
+            sent, sent_to = pick2(1 - c, s, PIECE_AT), pick2(1 - c, s + 1, PIECE_AT)
+            own_at, own_to = pick2(c, s, PIECE_AT), pick2(c, s + 1, PIECE_AT)
+
+            def at_piece(side, n):
+                code = packed(side, n, [[t * 4 + k for t, k in p] for p in PIECES])
+                tile, k = lax.div(code, 4), lax.rem(code, 4)
+                kind = pick(tile, [a * 8 + b * 2 + full for a, b, full in TILES])
+                return tile, k, lax.div(kind, 8), lax.rem(lax.div(kind, 2), 4), lax.rem(kind, 2)
+
+            def turn(n):
+                @pl.when(sent + n < sent_to)
                 def _():
-                    product(a, b, full, k, ch)
-                    send_part(sent, tile, k)
-
-                return sent + jnp.where(ch != c, 1, 0)
-
-            def mine(n):
-                tile, k, ch, a, b, full = at_piece(n)
-
-                @pl.when(ch == c)
+                    tile, k, a, b, full = at_piece(1 - c, sent + n)
+                    theirs(sent + n, a, b, full, k)
+
+                @pl.when((n >= LAG) & (own_at + n - LAG < own_to))
                 def _():
-                    product(a, b, full, k, ch)
-                    settle(tile, k)
-
-            def before(n):
-                total = jnp.int32(0)
-                for m, p in enumerate(PIECES):
-                    total = total + jnp.where((m < n) & (p[2] != c), 1, 0)
-                return total
-
-            lax.fori_loop(first, last, other, before(first))
-            many(first, last, mine)
+                    tile, k, a, b, full = at_piece(c, own_at + n - LAG)
+                    settle(own_at + n - LAG, COUNT, tile, a, b, full, k)
+
+            many(0, jnp.maximum(sent_to - sent, own_to - own_at + LAG), turn)
 
             def yd_in(n):
-                j = pick(n, [i[0] for i in YD])
-                kk = pick(n, [i[1] for i in YD])
+                j = pick2(c, n, [[i[0] for i in items] for items in YD])
+                kk = pick2(c, n, [[i[1] for i in items] for items in YD])
                 yd(j, kk).wait_recv()
                 value = keepd[j, rows(kk)] + decode(yrd[j, rows(kk)])
 
@@ -479,23 +494,25 @@
                     yrd[j, rows(kk)] = encode(value)
                     xd(j // 2, kk, j).start()
 
-            many(pick(s, YD_AT), pick(s + 1, YD_AT), yd_in)
+            many(pick2(c, s, YD_AT), pick2(c, s + 1, YD_AT), yd_in)
 
             def xd_in(n):
-                t = pick(n, [i[0] for i in XD])
-                kk = pick(n, [i[1] for i in XD])
+                t = pick2(c, n, [[i[0] for i in items] for items in XD])
+                kk = pick2(c, n, [[i[1] for i in items] for items in XD])
                 xd(t, kk, 0).wait_recv()
                 value = keepd[2 * t + X, rows(kk)] + decode(xrd[t, rows(kk)])
                 xrd[t, rows(kk)] = encode(value)
                 zd(t, kk).start()
 
-            many(pick(s, XD_AT), pick(s + 1, XD_AT), xd_in)
+            many(pick2(c, s, XD_AT), pick2(c, s + 1, XD_AT), xd_in)
 
         many(0, LAST + 1, slot_step)
 
         def pass_on(kk):
             zd(1, kk).wait_recv()
-            forward(kk).start()
+            value = keepg[rows(kk)] + decode(din[1, rows(kk)])
+            drecv[9 + X, rows(2 * Y + kk)] = encode(value)
+            grow(2 + X, 2 * Y + kk).start()
 
         def wait_din():
             many(0, 2, pass_on)
@@ -516,28 +533,23 @@
             zd(n // 2, n % 2).wait_send()
 
         many(0, 4, ends4)
-        many(0, 2, lambda kk: forward(kk).wait_send())
         many(0, 12, lambda n: grow(1 + n // 4, n % 4).wait_send())
 
     @pl.when(outer)
     def _():
-        def other(k):
-            product(0, 0, jnp.int32(1), k, 1 - c)
-            send_part(k, jnp.int32(0), k)
-
-        def mine(k):
-            product(0, 0, jnp.int32(1), k, c)
-            settle(jnp.int32(0), k)
-
-        many(0, 4, other)
-        many(0, 4, mine)
+        many(0, 4, lambda k: theirs(k, 0, 0, jnp.int32(1), k))
+        many(0, 4, lambda k: settle(k, 4, jnp.int32(0), 0, 0, jnp.int32(1), k))
 
         def arrived(n):
-            j = pick(n, [i[0] for i in G_ORDER])
-            k = pick(n, [i[1] for i in G_ORDER])
-            grow(j, k).wait_recv()
-
-            @pl.when(j % 2 == X)
+            j = pick2(c, n, [[i[0] for i in G_ORDER[ch]] for ch in range(2)])
+            k = pick2(c, n, [[i[1] for i in G_ORDER[ch]] for ch in range(2)])
+            later = (j == 2 + X) & (k // 2 == Y)
+
+            @pl.when(jnp.logical_not(later))
+            def _():
+                grow(j, k).wait_recv()
+
+            @pl.when((j % 2 == X) & jnp.logical_not(later))
             def _():
                 kept(j, k, decode(drecv[j, rows(k)]))
 
@@ -545,8 +557,13 @@
             def _():
                 xt(j // 2, k, j).start()
 
+        def arrived_last(kk):
+            j, k = 2 + X, 2 * Y + kk
+            grow(j, k).wait_recv()
+            kept(j, k, decode(drecv[j, rows(k)]))
+
         many(0, 12, arrived)
-        last_stages(lambda: many(0, 2, lambda kk: forward(kk).wait_recv()))
+        last_stages(lambda: many(0, 2, arrived_last))
         finish_ring()
         wait_sends()
         many(0, ARRIVALS, lambda n: inward(n)[0].wait_send())
@@ -557,7 +574,7 @@
     pairs, width = densities.shape
     rb, hw = width // 4, width // 2
     dma = pltpu.SemaphoreType.DMA
-    counts = (8, 8, 8, 8, RING, 44, 8, 8, 4, 4, 8, 8, 4, 4, 4, 4, 2, 2, 12, 12)
+    counts = (8, 8, 8, 8, SENDS, RING, 8, 8, 4, 4, 8, 8, 4, 4, 4, 4, 12, 12)
     return pl.pallas_call(
         kernel,
         out_shape=jax.ShapeDtypeStruct((width, hw), F32),
@@ -570,17 +587,19 @@
             pltpu.VMEM((4, pairs, width), BF16),
             pltpu.VMEM((4, width, pairs), BF16),
             pltpu.VMEM((11, width, hw), I16),
-            pltpu.VMEM((RING, rb, hw), I16),
+            pltpu.VMEM((SENDS, rb, hw), F32),
+            pltpu.VMEM((RING, rb, hw), F32),
             pltpu.VMEM((rb, hw), F32),
             pltpu.VMEM((2, width, hw), F32),
             pltpu.VMEM((4, hw, hw), F32),
+            pltpu.VMEM((hw, hw), F32),
             pltpu.VMEM((2, width, hw), I16),
             pltpu.VMEM((width, hw), I16),
             pltpu.VMEM((4, hw, hw), I16),
             pltpu.VMEM((2, hw, hw), I16),
             pltpu.VMEM((2, hw, hw), I16),
-            pltpu.VMEM((8, 128), I16),
             dma,
+            pltpu.SemaphoreType.REGULAR,
         ]
         + [dma((n,)) for n in counts],
         compiler_params=pltpu.CompilerParams(

time: 178 us -> 147 us (0.83)
  the two profiles are of different devices: /device:TPU:7 before, /device:TPU:5 now
where the time goes in v1:
time: 147 us; the launch traced here: 146 us
  Pallas kernels  140 us (95%)
  local copies, waits for them, and re-layouts  3.68 us (3%)
  other arithmetic  2.43 us (2%)
    pallas_call x1, Pallas kernels, one_kernel(): pl.pallas_call(kernel, out_shape=jax.ShapeDtypeStruct((width, hw), F32),...  140 us
    unnamed x1, local copies, waits for them, and re-layouts  3.08 us

profile of v1, /device:TPU:5, one launch (start us, length us, event | category | flops | bytes accessed | tf_op | source)
XLA Modules:
  0.0 146.5 jit_solution(4422760555478320141)
XLA Ops:
  0.0 1.2 select_reduce_fusion.1
  1.2 1.2 select_reduce_fusion
  2.4 0.6 div.18.weight
  3.0 140.3 %shard_map.55 = f32[1024,512]{1,0:T(8,128)} custom-call(bf16[1536,1024]{1,0:T(8,128)(2,1)} %dens.1, f32[1,1536]{1,0:T(1,128)} %div.18.weight), custom_call_target="tpu_custom_call" | custom-call | tf_op jit(solution)/shard_map/pallas_call | solution.py:578
  143.4 3.1 %copy.7 = f32[1024,512]{1,0:T(8,128)} copy(f32[1024,512]{1,0:T(8,128)} %shard_map.55) | data formatting | bytes 4194304
  (1 shorter events, 0.0 us)

commit v2 on v1

--- a/solution.py
+++ b/solution.py
@@ -106,7 +106,7 @@
 
 
 def order(items, slot):
-    items = sorted(items, key=lambda i: (slot(*i), i))
+    items = sorted(items, key=lambda i: (slot(*i), items.index(i)))
     return items, ranges([slot(*i) for i in items])
 
 
@@ -123,8 +123,8 @@
     return [f[0] for f in found], [f[1] for f in found]
 
 
-YD, YD_AT = both([(j, kk) for j in range(4) for kk in range(2)], yd_slot)
-XD, XD_AT = both([(t, kk) for t in range(2) for kk in range(2)], xd_slot)
+YD, YD_AT = both([(j, kk) for j in (2, 3, 0, 1) for kk in range(2)], yd_slot)
+XD, XD_AT = both([(t, kk) for t in (1, 0) for kk in range(2)], xd_slot)
 PIECE_AT = [ranges([piece_slot(*p, ch) for p in PIECES[ch]]) for ch in range(2)]
 G_ORDER = [[(t - 7, k) for t, k in PIECES[ch] if t >= 8] for ch in range(2)]
 
@@ -163,7 +163,7 @@
 
 
 def kernel(
-    dens, weight, out, mb, st, drecv, dsend, ring, acc, keep, keepd, keepg, xr, yr, yrd, xrd, din,
+    dens, val_band, cond_band, val_energy, cond_energy, out, mb, st, weight, drecv, dsend, ring, acc, keep, keepd, keepg, xr, yr, yrd, xrd, din,
     load_sem, credit, in_s, in_r, mid_s, mid_r, p_s, p_r, xt_s, xt_r, yt_s, yt_r,
     yd_s, yd_r, xd_s, xd_r, zd_s, zd_r, g_s, g_r,
 ):
@@ -227,6 +227,12 @@
     def _():
         pl.semaphore_wait(barrier, 4)
 
+    def slot_of(block):
+        return jnp.minimum(block, 2)
+
+    def place_of(block):
+        return jnp.where(block == 3, give_off, keep_off)
+
     def inward(n):
         kind = pick(n, [i[0] for i in INWARD])
         k = pick(n, [i[1] for i in INWARD])
@@ -244,16 +250,14 @@
 
     def relay(k):
         return remote(
-            mb.at[1, part(give_off), columns(k)], mb.at[3, part(give_off), columns(k)],
+            mb.at[1, part(give_off), columns(k)], mb.at[2, part(keep_off), columns(k)],
             mid_s.at[4 + k], mid_r.at[4 + k], to_cross,
         )
 
     def middle_in(n):
         block, k = 2 + n // 4, n % 4
-        return remote(
-            mb.at[block, part(keep_off), columns(k)], mb.at[block, part(keep_off), columns(k)],
-            mid_s.at[n], mid_r.at[n], to_cross,
-        ), block, k
+        place = mb.at[2, part(place_of(block)), columns(k)]
+        return remote(place, place, mid_s.at[n], mid_r.at[n], to_cross), block, k
 
     def swap(n):
         return remote(
@@ -292,11 +296,12 @@
             drecv.at[7 + j, rows(k)], drecv.at[j, rows(k)], g_s.at[n], g_r.at[n], to_mate
         )
 
-    def transpose(block, off, k):
+    def transpose(slot, place, off, k):
         def step(n):
-            r = pl.ds(pl.multiple_of(off + n * kb, kb), kb)
-            t = mb[block, r, columns(k)].T
-            st[block, columns(k), r] = (t.astype(F32) * weight[:, r]).astype(BF16)
+            r = pl.ds(pl.multiple_of(place + n * kb, kb), kb)
+            w = weight[:, pl.ds(pl.multiple_of(off + n * kb, kb), kb)]
+            t = mb[slot, r, columns(k)].T
+            st[slot, columns(k), r] = (t.astype(F32) * w).astype(BF16)
 
         many(0, half // kb, step)
 
@@ -304,7 +309,8 @@
         @pl.when(full == 0)
         def _():
             put(jnp.dot(
-                st[a, rows(k), part(keep_off)], mb[b, part(keep_off), sides(ch)],
+                st[slot_of(a), rows(k), part(place_of(a))],
+                mb[slot_of(b), part(place_of(b)), sides(ch)],
                 preferred_element_type=F32,
             ))
 
@@ -326,11 +332,20 @@
         many(0, 4, lambda k: across(k).start())
 
     load.start()
+
+    def level(bands, table):
+        size = table.shape[0]
+        column = jnp.broadcast_to(table[...].reshape(1, size), (8, size)).T[:, :1]
+        found = lax.broadcasted_iota(jnp.int32, (size, pairs), 0) == bands[...].reshape(1, pairs)
+        return jnp.sum(jnp.where(found, column, 0.0), axis=0, keepdims=True)
+
+    gap = level(val_band, val_energy) - level(cond_band, cond_energy)
+    weight[...] = 4.0 / (gap * math.sqrt(pairs * lax.axis_size("pair")))
     load.wait()
 
     def own(k):
-        transpose(0, keep_off, k)
-        transpose(0, give_off, k)
+        transpose(0, keep_off, keep_off, k)
+        transpose(0, give_off, give_off, k)
 
     many(0, 4, own)
 
@@ -447,7 +462,7 @@
                 n = s - 1
                 copy, block, k = middle_in(n)
                 copy.wait_recv()
-                transpose(block, keep_off, k)
+                transpose(2, place_of(block), keep_off, k)
                 copy, kind, k, off = inward(n)
                 copy.wait_recv()
 
@@ -455,7 +470,7 @@
                 def _():
                     relay(k).start()
 
-                transpose(1, off, k)
+                transpose(1, off, off, k)
 
             sent, sent_to = pick2(1 - c, s, PIECE_AT), pick2(1 - c, s + 1, PIECE_AT)
             own_at, own_to = pick2(c, s, PIECE_AT), pick2(c, s + 1, PIECE_AT)
@@ -570,22 +585,22 @@
 
 
 def one_kernel(densities, *bands):
-    weight = weights(densities, *bands)[None, :]
     pairs, width = densities.shape
     rb, hw = width // 4, width // 2
     dma = pltpu.SemaphoreType.DMA
     counts = (8, 8, 8, 8, SENDS, RING, 8, 8, 4, 4, 8, 8, 4, 4, 4, 4, 12, 12)
     return pl.pallas_call(
         kernel,
-        out_shape=jax.ShapeDtypeStruct((width, hw), F32),
+        out_shape=pltpu.VMEM((width, hw), F32),
         in_specs=[
             pl.BlockSpec(memory_space=pl.ANY),
-            pl.BlockSpec(memory_space=pltpu.VMEM),
-        ],
+        ]
+        + [pl.BlockSpec(memory_space=pltpu.VMEM)] * 4,
         out_specs=pl.BlockSpec(memory_space=pltpu.VMEM),
         scratch_shapes=[
-            pltpu.VMEM((4, pairs, width), BF16),
-            pltpu.VMEM((4, width, pairs), BF16),
+            pltpu.VMEM((3, pairs, width), BF16),
+            pltpu.VMEM((3, width, pairs), BF16),
+            pltpu.VMEM((1, pairs), F32),
             pltpu.VMEM((11, width, hw), I16),
             pltpu.VMEM((SENDS, rb, hw), F32),
             pltpu.VMEM((RING, rb, hw), F32),
@@ -603,9 +618,9 @@
         ]
         + [dma((n,)) for n in counts],
         compiler_params=pltpu.CompilerParams(
-            collective_id=0, has_side_effects=True, vmem_limit_bytes=62 * 2**20
+            collective_id=0, has_side_effects=True, vmem_limit_bytes=58 * 2**20
         ),
-    )(densities, weight)
+    )(densities, *bands)
 
 
 def solution(mesh):

time: 147 us -> 141 us (0.959)
  other arithmetic: 2.43 us -> 0 us
  local copies, waits for them, and re-layouts: 3.68 us -> 1.32 us
    reduce_sum x2 -> x0, other arithmetic: 2.42 us -> none  [lookup(): return jnp.sum(onehot * table[None, :], axis=1)]
    unnamed x1, local copies, waits for them, and re-layouts: 3.08 us -> 1.32 us
where the time goes in v2:
time: 141 us
  Pallas kernels  139 us (99%)
    pallas_call x1, Pallas kernels, one_kernel(): pl.pallas_call(kernel, out_shape=pltpu.VMEM((width, hw), F32), in_specs=[...  139 us

profile of v2, /device:TPU:5, one launch (start us, length us, event | category | flops | bytes accessed | tf_op | source)
XLA Modules:
  0.0 140.5 jit_solution(11694178993410970488)
XLA Ops:
  0.0 139.2 %shard_map.55 = f32[1024,512]{1,0:T(8,128)S(1)} custom-call(bf16[1536,1024]{1,0:T(8,128)(2,1)} %dens.1, s32[1536]{0:T(1024)} %val_band.1, s32[1536]{0:T(1024)} %cond_band.1, f32[128]{0:T(128)} %val_energy.1, f32[256]{0:T(256)} %cond_energy.1), custom_call_target="tpu_custom_call" | custom-call | tf_op jit(solution)/shard_map/pallas_call | solution.py:592
  139.2 1.3 copy.7

commit v3 on v2

--- a/solution.py
+++ b/solution.py
@@ -63,70 +63,49 @@
     (2, 1, 0), (2, 0, 0), (3, 1, 0), (3, 0, 0),
     (1, 0, 1), (1, 2, 0), (1, 3, 0),
 )
-INWARD = ((0, 0), (0, 1), (1, 0), (1, 1), (1, 2), (1, 3), (0, 2), (0, 3))
+INWARD = ((0, 0), (1, 0), (0, 1), (1, 1), (0, 2), (1, 2), (1, 3), (0, 3))
 ARRIVALS = 8
-RING, SENDS, LAG = 8, 4, 2
-
-
-def chunk_slot(block, k, full):
-    if block == 0:
-        return 0
-    if block == 1:
-        slots = [INWARD.index((0, k)) + 1]
-        if full:
-            slots.append(INWARD.index((1, k)) + 1)
-        return max(slots)
-    return (block - 2) * 4 + k + 1
-
-
-def piece_slot(tile, k, ch):
-    a, b, full = TILES[tile]
-    columns = max(chunk_slot(b, 2 * ch, full), chunk_slot(b, 2 * ch + 1, full))
-    slot = max(chunk_slot(a, k, full), columns)
-    if slot == ARRIVALS and not 4 <= tile < 8:
-        slot += 1 if tile >= 8 else 2
-    return slot
-
-
-PRIORITY = (6, 7, 4, 5, 10, 9, 8, 3, 0, 2, 1)
-PIECES = [
-    sorted(
-        ((t, k) for t in range(11) for k in range(4)),
-        key=lambda p: (piece_slot(*p, ch), PRIORITY.index(p[0]), p[1]),
-    )
-    for ch in range(2)
-]
+RING, SENDS = 8, 4
 COUNT = 44
-LAST = ARRIVALS + 4
-
-
-def ranges(slots):
-    slots = sorted(slots)
-    return [sum(1 for s in slots if s < n) for n in range(LAST + 2)]
-
-
-def order(items, slot):
-    items = sorted(items, key=lambda i: (slot(*i), items.index(i)))
-    return items, ranges([slot(*i) for i in items])
-
-
-def yd_slot(ch, j, kk):
-    return max(piece_slot(4 + j, 2 * v + kk, ch) for v in (0, 1)) + 1
-
-
-def xd_slot(ch, t, kk):
-    return max(ARRIVALS, *(yd_slot(ch, 2 * t + x, kk) for x in (0, 1))) + 1
-
-
-def both(items, slot):
-    found = [order(items, functools.partial(slot, ch)) for ch in range(2)]
-    return [f[0] for f in found], [f[1] for f in found]
-
-
-YD, YD_AT = both([(j, kk) for j in (2, 3, 0, 1) for kk in range(2)], yd_slot)
-XD, XD_AT = both([(t, kk) for t in (1, 0) for kk in range(2)], xd_slot)
-PIECE_AT = [ranges([piece_slot(*p, ch) for p in PIECES[ch]]) for ch in range(2)]
-G_ORDER = [[(t - 7, k) for t, k in PIECES[ch] if t >= 8] for ch in range(2)]
+PIECES = (
+    (
+        4, 7, 5, 36, 9, 6, 10, 20, 22, 32, 23, 17, 3, 2, 21, 19, 0, 33, 38, 18, 26, 16, 30, 34,
+        1, 27, 31, 24, 11, 28, 40, 25, 14, 42, 29, 43, 15, 39, 35, 37, 12, 41, 13, 8,
+    ),
+    (
+        6, 7, 5, 4, 22, 32, 8, 20, 33, 37, 23, 38, 41, 10, 31, 30, 42, 40, 11, 21, 13, 34, 9, 36,
+        28, 12, 14, 35, 39, 27, 3, 26, 43, 19, 24, 25, 29, 2, 17, 18, 1, 16, 15, 0,
+    ),
+)
+INNER = (
+    (
+        0, 3, 2, 1, 1, 1, 0, 0, 2, 1, 1, 1, 2, 0, 0, 25, 1, 2, 3, 1, 3, 1, 0, 1,
+        0, 0, 3, 2, 0, 1, 1, 0, 1, 1, 1, 1, 1, 23, 0, 1, 3, 1, 1, 0, 2, 0, 6, 1,
+        0, 0, 1, 3, 0, 0, 7, 0, 0, 20, 5, 1, 0, 0, 1, 28, 1, 22, 0, 2, 21, 0, 4, 0,
+        3, 0, 0, 1, 1, 13, 0, 3, 0, 2, 0, 0, 1, 1, 0, 0, 1, 12, 0, 1, 1, 0, 1, 1,
+        1, 0, 0, 8, 1, 0, 1, 1, 0, 9, 11, 10, 1, 0, 1, 0, 0, 1, 15, 1, 1, 33, 0, 14,
+        19, 0, 32, 18, 0, 24, 29, 16, 1, 17, 35, 31, 37, 27, 30, 36, 34, 26,
+    ),
+    (
+        0, 0, 0, 2, 3, 2, 1, 0, 0, 0, 3, 1, 0, 0, 2, 25, 24, 0, 1, 3, 1, 2, 0, 1,
+        0, 0, 3, 0, 0, 0, 1, 1, 1, 0, 0, 3, 0, 0, 0, 2, 1, 0, 0, 1, 3, 2, 1, 1,
+        1, 0, 6, 1, 0, 0, 0, 1, 1, 23, 3, 1, 0, 1, 1, 1, 1, 1, 1, 2, 1, 1, 0, 1,
+        0, 3, 0, 1, 1, 2, 0, 0, 1, 7, 0, 0, 32, 0, 0, 28, 1, 1, 0, 10, 1, 0, 0, 1,
+        27, 31, 1, 1, 1, 1, 0, 0, 0, 1, 0, 8, 29, 9, 1, 0, 22, 1, 1, 11, 26, 1, 17, 14,
+        30, 1, 20, 5, 16, 15, 19, 4, 33, 21, 13, 12, 35, 1, 18, 37, 36, 34,
+    ),
+)
+OUTER = (
+    (
+        0, 8, 0, 0, 0, 5, 10, 4, 1, 18, 1, 23, 6, 1, 22, 12, 24, 28, 20, 1, 19, 14, 15, 11,
+        32, 9, 7, 25, 21, 33, 13, 29, 16, 26, 30, 36, 34, 17, 31, 27, 37, 35,
+    ),
+    (
+        1, 0, 0, 14, 18, 12, 5, 4, 1, 13, 0, 1, 0, 23, 22, 1, 9, 32, 21, 10, 11, 15, 20, 28,
+        6, 29, 33, 8, 19, 24, 17, 31, 27, 16, 30, 7, 26, 25, 34, 35, 37, 36,
+    ),
+)
+NOTHING = 63
 
 
 def pick(index, values):
@@ -208,8 +187,10 @@
     def part(off):
         return pl.ds(pl.multiple_of(off, half), half)
 
+    side = (c + h) % 2
+
     def columns(k):
-        return pl.ds(pl.multiple_of(k * rb, rb), rb)
+        return pl.ds(pl.multiple_of((k + 2 * h) % 4 * rb, rb), rb)
 
     def sides(k):
         return pl.ds(pl.multiple_of(k * hw, hw), hw)
@@ -244,7 +225,7 @@
 
     def across(k):
         return remote(
-            dens.at[part(give_off), columns(k)], mb.at[2, part(give_off), columns(k)],
+            dens.at[part(give_off), columns(k + 2)], mb.at[2, part(give_off), columns(k + 2)],
             mid_s.at[k], mid_r.at[k], to_cross,
         )
 
@@ -255,7 +236,7 @@
         )
 
     def middle_in(n):
-        block, k = 2 + n // 4, n % 4
+        block, k = 2 + n // 4, (n + 2 * (n // 4)) % 4
         place = mb.at[2, part(place_of(block)), columns(k)]
         return remote(place, place, mid_s.at[n], mid_r.at[n], to_cross), block, k
 
@@ -274,7 +255,7 @@
 
     def yd(j, kk):
         return remote(
-            drecv.at[4 + j, rows(2 * Y + kk)], yrd.at[j, rows(kk)],
+            drecv.at[4 + j, rows(2 * (1 - Y) + kk)], yrd.at[j, rows(kk)],
             yd_s.at[j * 2 + kk], yd_r.at[j * 2 + kk], to_y,
         )
 
@@ -301,7 +282,7 @@
             r = pl.ds(pl.multiple_of(place + n * kb, kb), kb)
             w = weight[:, pl.ds(pl.multiple_of(off + n * kb, kb), kb)]
             t = mb[slot, r, columns(k)].T
-            st[slot, columns(k), r] = (t.astype(F32) * w).astype(BF16)
+            st[slot, rows(k), r] = (t.astype(F32) * w).astype(BF16)
 
         many(0, half // kb, step)
 
@@ -380,7 +361,7 @@
         def _():
             kept(tile, k, acc[...])
 
-        stays = (tile >= 4) & (tile < 8) & (k // 2 != Y)
+        stays = (tile >= 4) & (tile < 8) & (k // 2 == Y)
 
         @pl.when(stays)
         def _():
@@ -418,6 +399,7 @@
 
         @pl.when(late)
         def _():
+            zd(0, k % 2).wait_recv()
             xr[1 - Y, rows(k)] = encode(value + decode(din[0, rows(k % 2)]))
 
         @pl.when(jnp.logical_not(late))
@@ -434,17 +416,12 @@
 
         @pl.when(late)
         def _():
-            out[rows(k)] = value + decode(din[0, rows(k % 2)])
+            zd(0, k % 2).wait_recv()
+            out[columns(k)] = value + decode(din[0, rows(k % 2)])
 
         @pl.when(jnp.logical_not(late))
         def _():
-            out[rows(k)] = value
-
-    def last_stages(wait_din):
-        many(0, 2, lambda n: give_y(2 * (1 - Y) * (1 - Y) + 2 * Y * (1 - Y) + n))
-        wait_din()
-        many(0, 2, lambda n: give_y(2 * Y + n))
-        many(0, 4, finish)
+            out[columns(k)] = value
 
     def wait_sends():
         def step(k):
@@ -454,86 +431,129 @@
 
         many(0, 4, step)
 
-    @pl.when(inner)
-    def _():
-        def slot_step(s):
-            @pl.when((s >= 1) & (s <= ARRIVALS))
+    def run(lists, step):
+        size = -(-max(map(len, lists)) // 5)
+        padded = [list(l) + [NOTHING] * (5 * size - len(l)) for l in lists]
+        words = [
+            [sum(v << (6 * i) for i, v in enumerate(l[n : n + 5])) for n in range(0, 5 * size, 5)]
+            for l in padded
+        ]
+
+        def one(i, state):
+            word, counts = state
+            code = lax.rem(word, 64)
+            step(code, counts)
+            counts = tuple(n + jnp.where(code == kind, 1, 0) for kind, n in enumerate(counts))
+            return lax.div(word, 64), counts
+
+        def five(w, counts):
+            return lax.fori_loop(0, 5, one, (pick2(side, w, words), counts))[1]
+
+        lax.fori_loop(0, size, five, (jnp.int32(0),) * 4)
+
+    def on(condition, body):
+        pl.when(condition)(body)
+
+    def late_steps(code):
+        n = code - 18
+        on((n >= 0) & (n < 16) & (lax.div(n, 4) == 2 * (1 - Y) + X), lambda: give_y(lax.rem(n, 4)))
+        on((code >= 34) & (code < 38), lambda: finish(code - 34))
+
+    def at_piece(whose, n):
+        code = packed(whose, n, PIECES)
+        tile, k = lax.div(code, 4), lax.rem(code, 4)
+        kind = pick(tile, [a * 8 + b * 2 + full for a, b, full in TILES])
+        return tile, k, lax.div(kind, 8), lax.rem(lax.div(kind, 2), 4), lax.rem(kind, 2)
+
+    def inner_step(code, counts):
+        def form_theirs():
+            tile, k, a, b, full = at_piece(1 - side, counts[0])
+            theirs(counts[0], a, b, full, k)
+
+        def form_own():
+            tile, k, a, b, full = at_piece(side, counts[1])
+            settle(counts[1], COUNT, tile, a, b, full, k)
+
+        def from_across():
+            copy, block, k = middle_in(counts[2])
+            copy.wait_recv()
+            transpose(2, place_of(block), keep_off, k)
+
+        def from_outside():
+            copy, kind, k, off = inward(counts[3])
+            copy.wait_recv()
+            on(kind == 1, lambda: relay(k).start())
+            transpose(1, off, off, k)
+
+        def yd_in():
+            j, kk = lax.div(code - 4, 2), lax.rem(code - 4, 2)
+            yd(j, kk).wait_recv()
+            value = keepd[j, rows(kk)] + decode(yrd[j, rows(kk)])
+
+            @pl.when(j % 2 == X)
             def _():
-                n = s - 1
-                copy, block, k = middle_in(n)
-                copy.wait_recv()
-                transpose(2, place_of(block), keep_off, k)
-                copy, kind, k, off = inward(n)
-                copy.wait_recv()
-
-                @pl.when(kind == 1)
-                def _():
-                    relay(k).start()
-
-                transpose(1, off, off, k)
-
-            sent, sent_to = pick2(1 - c, s, PIECE_AT), pick2(1 - c, s + 1, PIECE_AT)
-            own_at, own_to = pick2(c, s, PIECE_AT), pick2(c, s + 1, PIECE_AT)
-
-            def at_piece(side, n):
-                code = packed(side, n, [[t * 4 + k for t, k in p] for p in PIECES])
-                tile, k = lax.div(code, 4), lax.rem(code, 4)
-                kind = pick(tile, [a * 8 + b * 2 + full for a, b, full in TILES])
-                return tile, k, lax.div(kind, 8), lax.rem(lax.div(kind, 2), 4), lax.rem(kind, 2)
-
-            def turn(n):
-                @pl.when(sent + n < sent_to)
-                def _():
-                    tile, k, a, b, full = at_piece(1 - c, sent + n)
-                    theirs(sent + n, a, b, full, k)
-
-                @pl.when((n >= LAG) & (own_at + n - LAG < own_to))
-                def _():
-                    tile, k, a, b, full = at_piece(c, own_at + n - LAG)
-                    settle(own_at + n - LAG, COUNT, tile, a, b, full, k)
-
-            many(0, jnp.maximum(sent_to - sent, own_to - own_at + LAG), turn)
-
-            def yd_in(n):
-                j = pick2(c, n, [[i[0] for i in items] for items in YD])
-                kk = pick2(c, n, [[i[1] for i in items] for items in YD])
-                yd(j, kk).wait_recv()
-                value = keepd[j, rows(kk)] + decode(yrd[j, rows(kk)])
-
-                @pl.when(j % 2 == X)
-                def _():
-                    keepd[j, rows(kk)] = value
-
-                @pl.when(j % 2 != X)
-                def _():
-                    yrd[j, rows(kk)] = encode(value)
-                    xd(j // 2, kk, j).start()
-
-            many(pick2(c, s, YD_AT), pick2(c, s + 1, YD_AT), yd_in)
-
-            def xd_in(n):
-                t = pick2(c, n, [[i[0] for i in items] for items in XD])
-                kk = pick2(c, n, [[i[1] for i in items] for items in XD])
-                xd(t, kk, 0).wait_recv()
-                value = keepd[2 * t + X, rows(kk)] + decode(xrd[t, rows(kk)])
-                xrd[t, rows(kk)] = encode(value)
-                zd(t, kk).start()
-
-            many(pick2(c, s, XD_AT), pick2(c, s + 1, XD_AT), xd_in)
-
-        many(0, LAST + 1, slot_step)
-
-        def pass_on(kk):
+                keepd[j, rows(kk)] = value
+
+            @pl.when(j % 2 != X)
+            def _():
+                yrd[j, rows(kk)] = encode(value)
+                xd(j // 2, kk, j).start()
+
+        def xd_in():
+            t, kk = lax.div(code - 12, 2), lax.rem(code - 12, 2)
+            xd(t, kk, 0).wait_recv()
+            value = keepd[2 * t + X, rows(kk)] + decode(xrd[t, rows(kk)])
+            xrd[t, rows(kk)] = encode(value)
+            zd(t, kk).start()
+
+        def pass_on():
+            kk = code - 16
             zd(1, kk).wait_recv()
             value = keepg[rows(kk)] + decode(din[1, rows(kk)])
             drecv[9 + X, rows(2 * Y + kk)] = encode(value)
             grow(2 + X, 2 * Y + kk).start()
 
-        def wait_din():
-            many(0, 2, pass_on)
-            many(0, 2, lambda kk: zd(0, kk).wait_recv())
-
-        last_stages(wait_din)
+        on(code == 0, form_theirs)
+        on(code == 1, form_own)
+        on(code == 2, from_across)
+        on(code == 3, from_outside)
+        on((code >= 4) & (code < 12), yd_in)
+        on((code >= 12) & (code < 16), xd_in)
+        on((code >= 16) & (code < 18), pass_on)
+        late_steps(code)
+
+    def outer_step(code, counts):
+        one = jnp.int32(1)
+        on(code == 0, lambda: theirs(counts[0], 0, 0, one, counts[0]))
+        on(code == 1, lambda: settle(counts[1], 4, jnp.int32(0), 0, 0, one, counts[1]))
+
+        def arrived():
+            j, k = 1 + lax.div(code - 4, 4), lax.rem(code - 4, 4)
+
+            @pl.when(jnp.logical_not((j == 2 + X) & (k // 2 == Y)))
+            def _():
+                grow(j, k).wait_recv()
+
+                @pl.when(j % 2 == X)
+                def _():
+                    kept(j, k, decode(drecv[j, rows(k)]))
+
+                @pl.when(j % 2 != X)
+                def _():
+                    xt(j // 2, k, j).start()
+
+        def arrived_last():
+            j, k = 2 + X, 2 * Y + code - 16
+            grow(j, k).wait_recv()
+            kept(j, k, decode(drecv[j, rows(k)]))
+
+        on((code >= 4) & (code < 16), arrived)
+        on((code >= 16) & (code < 18), arrived_last)
+        late_steps(code)
+
+    @pl.when(inner)
+    def _():
+        run(INNER, inner_step)
         finish_ring()
         wait_sends()
 
@@ -552,33 +572,7 @@
 
     @pl.when(outer)
     def _():
-        many(0, 4, lambda k: theirs(k, 0, 0, jnp.int32(1), k))
-        many(0, 4, lambda k: settle(k, 4, jnp.int32(0), 0, 0, jnp.int32(1), k))
-
-        def arrived(n):
-            j = pick2(c, n, [[i[0] for i in G_ORDER[ch]] for ch in range(2)])
-            k = pick2(c, n, [[i[1] for i in G_ORDER[ch]] for ch in range(2)])
-            later = (j == 2 + X) & (k // 2 == Y)
-
-            @pl.when(jnp.logical_not(later))
-            def _():
-                grow(j, k).wait_recv()
-
-            @pl.when((j % 2 == X) & jnp.logical_not(later))
-            def _():
-                kept(j, k, decode(drecv[j, rows(k)]))
-
-            @pl.when(j % 2 != X)
-            def _():
-                xt(j // 2, k, j).start()
-
-        def arrived_last(kk):
-            j, k = 2 + X, 2 * Y + kk
-            grow(j, k).wait_recv()
-            kept(j, k, decode(drecv[j, rows(k)]))
-
-        many(0, 12, arrived)
-        last_stages(lambda: many(0, 2, arrived_last))
+        run(OUTER, outer_step)
         finish_ring()
         wait_sends()
         many(0, ARRIVALS, lambda n: inward(n)[0].wait_send())

time: 141 us -> 131 us (0.929)
  the two profiles are of different devices: /device:TPU:5 before, /device:TPU:14 now
where the time goes in v3:
time: 131 us
  Pallas kernels  130 us (99%)
  local copies, waits for them, and re-layouts  1.32 us (1%)
    pallas_call x1, Pallas kernels, one_kernel(): pl.pallas_call(kernel, out_shape=pltpu.VMEM((width, hw), F32), in_specs=[...  130 us

profile of v3, /device:TPU:14, one launch (start us, length us, event | category | flops | bytes accessed | tf_op | source)
XLA Modules:
  0.0 131.1 jit_solution(3082735745465076066)
XLA Ops:
  0.0 129.8 %shard_map.55 = f32[1024,512]{1,0:T(8,128)S(1)} custom-call(bf16[1536,1024]{1,0:T(8,128)(2,1)} %dens.1, s32[1536]{0:T(1024)} %val_band.1, s32[1536]{0:T(1024)} %cond_band.1, f32[128]{0:T(128)} %val_energy.1, f32[256]{0:T(256)} %cond_energy.1), custom_call_target="tpu_custom_call" | custom-call | tf_op jit(solution)/shard_map/pallas_call | solution.py:586
  129.8 1.3 %copy.7 = f32[1024,512]{1,0:T(8,128)} copy(f32[1024,512]{1,0:T(8,128)S(1)} %shard_map.55) | data formatting | bytes 4194304

commit v4 on v3

--- a/solution.py
+++ b/solution.py
@@ -69,40 +69,40 @@
 COUNT = 44
 PIECES = (
     (
-        4, 7, 5, 36, 9, 6, 10, 20, 22, 32, 23, 17, 3, 2, 21, 19, 0, 33, 38, 18, 26, 16, 30, 34,
-        1, 27, 31, 24, 11, 28, 40, 25, 14, 42, 29, 43, 15, 39, 35, 37, 12, 41, 13, 8,
+        5, 6, 20, 4, 11, 36, 10, 32, 21, 16, 17, 8, 7, 19, 33, 0, 23, 2, 3, 38, 18, 1, 37, 22,
+        34, 30, 26, 31, 27, 28, 24, 40, 29, 42, 35, 12, 25, 43, 15, 39, 41, 13, 9, 14,
     ),
     (
-        6, 7, 5, 4, 22, 32, 8, 20, 33, 37, 23, 38, 41, 10, 31, 30, 42, 40, 11, 21, 13, 34, 9, 36,
-        28, 12, 14, 35, 39, 27, 3, 26, 43, 19, 24, 25, 29, 2, 17, 18, 1, 16, 15, 0,
+        20, 7, 4, 6, 22, 32, 21, 5, 10, 33, 9, 36, 23, 38, 30, 11, 37, 40, 41, 15, 14, 31, 8, 42,
+        34, 13, 28, 39, 24, 26, 18, 43, 1, 16, 27, 29, 35, 19, 25, 2, 12, 17, 3, 0,
     ),
 )
 INNER = (
     (
-        0, 3, 2, 1, 1, 1, 0, 0, 2, 1, 1, 1, 2, 0, 0, 25, 1, 2, 3, 1, 3, 1, 0, 1,
-        0, 0, 3, 2, 0, 1, 1, 0, 1, 1, 1, 1, 1, 23, 0, 1, 3, 1, 1, 0, 2, 0, 6, 1,
-        0, 0, 1, 3, 0, 0, 7, 0, 0, 20, 5, 1, 0, 0, 1, 28, 1, 22, 0, 2, 21, 0, 4, 0,
-        3, 0, 0, 1, 1, 13, 0, 3, 0, 2, 0, 0, 1, 1, 0, 0, 1, 12, 0, 1, 1, 0, 1, 1,
-        1, 0, 0, 8, 1, 0, 1, 1, 0, 9, 11, 10, 1, 0, 1, 0, 0, 1, 15, 1, 1, 33, 0, 14,
-        19, 0, 32, 18, 0, 24, 29, 16, 1, 17, 35, 31, 37, 27, 30, 36, 34, 26,
+        3, 2, 1, 1, 0, 0, 1, 3, 1, 0, 2, 1, 24, 2, 1, 0, 3, 1, 0, 1, 1, 1, 1, 1,
+        1, 0, 29, 0, 0, 23, 2, 0, 1, 3, 0, 0, 0, 1, 0, 1, 3, 1, 1, 2, 25, 0, 0, 1,
+        0, 1, 1, 7, 0, 5, 3, 2, 0, 1, 18, 0, 22, 0, 1, 1, 0, 0, 1, 0, 0, 20, 3, 1,
+        1, 0, 1, 1, 6, 2, 1, 0, 0, 1, 3, 0, 0, 0, 13, 0, 4, 0, 0, 2, 1, 28, 10, 8,
+        1, 0, 12, 1, 0, 0, 1, 0, 0, 1, 1, 1, 0, 14, 1, 21, 11, 0, 9, 1, 0, 33, 0, 0,
+        16, 15, 30, 1, 1, 0, 1, 19, 1, 26, 17, 27, 35, 37, 34, 31, 32, 36,
     ),
     (
-        0, 0, 0, 2, 3, 2, 1, 0, 0, 0, 3, 1, 0, 0, 2, 25, 24, 0, 1, 3, 1, 2, 0, 1,
-        0, 0, 3, 0, 0, 0, 1, 1, 1, 0, 0, 3, 0, 0, 0, 2, 1, 0, 0, 1, 3, 2, 1, 1,
-        1, 0, 6, 1, 0, 0, 0, 1, 1, 23, 3, 1, 0, 1, 1, 1, 1, 1, 1, 2, 1, 1, 0, 1,
-        0, 3, 0, 1, 1, 2, 0, 0, 1, 7, 0, 0, 32, 0, 0, 28, 1, 1, 0, 10, 1, 0, 0, 1,
-        27, 31, 1, 1, 1, 1, 0, 0, 0, 1, 0, 8, 29, 9, 1, 0, 22, 1, 1, 11, 26, 1, 17, 14,
-        30, 1, 20, 5, 16, 15, 19, 4, 33, 21, 13, 12, 35, 1, 18, 37, 36, 34,
+        3, 2, 0, 0, 3, 0, 1, 0, 1, 2, 0, 0, 0, 3, 0, 25, 0, 2, 0, 0, 0, 0, 1, 1,
+        2, 1, 0, 3, 22, 1, 0, 0, 0, 1, 0, 0, 1, 1, 3, 1, 0, 24, 0, 1, 1, 1, 2, 1,
+        0, 0, 1, 0, 1, 1, 3, 0, 0, 23, 2, 1, 6, 0, 1, 1, 0, 1, 7, 1, 0, 2, 0, 1,
+        1, 1, 0, 3, 2, 0, 0, 0, 1, 3, 1, 0, 1, 0, 1, 1, 1, 1, 0, 10, 1, 0, 1, 0,
+        28, 8, 27, 0, 1, 14, 4, 1, 1, 0, 12, 1, 1, 11, 33, 26, 1, 0, 1, 1, 20, 9, 29, 0,
+        16, 0, 5, 1, 17, 31, 32, 15, 13, 19, 21, 1, 37, 35, 18, 30, 36, 34,
     ),
 )
 OUTER = (
     (
-        0, 8, 0, 0, 0, 5, 10, 4, 1, 18, 1, 23, 6, 1, 22, 12, 24, 28, 20, 1, 19, 14, 15, 11,
-        32, 9, 7, 25, 21, 33, 13, 29, 16, 26, 30, 36, 34, 17, 31, 27, 37, 35,
+        1, 8, 4, 0, 0, 1, 9, 0, 22, 10, 5, 18, 19, 6, 12, 0, 28, 23, 14, 1, 20, 7, 1, 24,
+        15, 32, 21, 11, 34, 16, 26, 29, 30, 25, 36, 33, 13, 17, 27, 31, 37, 35,
     ),
     (
-        1, 0, 0, 14, 18, 12, 5, 4, 1, 13, 0, 1, 0, 23, 22, 1, 9, 32, 21, 10, 11, 15, 20, 28,
-        6, 29, 33, 8, 19, 24, 17, 31, 27, 16, 30, 7, 26, 25, 34, 35, 37, 36,
+        0, 0, 0, 1, 1, 0, 4, 12, 5, 10, 6, 28, 18, 22, 19, 14, 1, 24, 20, 13, 11, 15, 1, 21,
+        23, 32, 7, 33, 29, 8, 16, 26, 9, 25, 17, 27, 30, 36, 34, 31, 37, 35,
     ),
 )
 NOTHING = 63

time: 131 us -> 129 us (0.985)
  the two profiles are of different devices: /device:TPU:14 before, /device:TPU:4 now
where the time goes in v4:
time: 129 us
  Pallas kernels  127 us (98%)
  local copies, waits for them, and re-layouts  1.32 us (1%)
    pallas_call x1, Pallas kernels, one_kernel(): pl.pallas_call(kernel, out_shape=pltpu.VMEM((width, hw), F32), in_specs=[...  127 us

profile of v4, /device:TPU:4, one launch (start us, length us, event | category | flops | bytes accessed | tf_op | source)
XLA Modules:
  0.0 128.5 jit_solution(14003976474166470745)
XLA Ops:
  0.0 127.2 %shard_map.55 = f32[1024,512]{1,0:T(8,128)S(1)} custom-call(bf16[1536,1024]{1,0:T(8,128)(2,1)} %dens.1, s32[1536]{0:T(1024)} %val_band.1, s32[1536]{0:T(1024)} %cond_band.1, f32[128]{0:T(128)} %val_energy.1, f32[256]{0:T(256)} %cond_energy.1), custom_call_target="tpu_custom_call" | custom-call | tf_op jit(solution)/shard_map/pallas_call | solution.py:586
  127.2 1.3 %copy.7 = f32[1024,512]{1,0:T(8,128)} copy(f32[1024,512]{1,0:T(8,128)S(1)} %shard_map.55) | data formatting | bytes 4194304

commit v5 on v4

--- a/solution.py
+++ b/solution.py
@@ -69,40 +69,112 @@
 COUNT = 44
 PIECES = (
     (
-        5, 6, 20, 4, 11, 36, 10, 32, 21, 16, 17, 8, 7, 19, 33, 0, 23, 2, 3, 38, 18, 1, 37, 22,
-        34, 30, 26, 31, 27, 28, 24, 40, 29, 42, 35, 12, 25, 43, 15, 39, 41, 13, 9, 14,
-    ),
-    (
-        20, 7, 4, 6, 22, 32, 21, 5, 10, 33, 9, 36, 23, 38, 30, 11, 37, 40, 41, 15, 14, 31, 8, 42,
-        34, 13, 28, 39, 24, 26, 18, 43, 1, 16, 27, 29, 35, 19, 25, 2, 12, 17, 3, 0,
+        7, 4, 6, 5, 11, 20, 21, 36, 37, 32, 18, 17, 22, 10, 8, 23, 16, 19, 33, 2, 3, 0, 26, 30,
+        1, 38, 27, 34, 24, 31, 28, 42, 25, 29, 39, 43, 35, 15, 40, 14, 41, 9, 13, 12,
+    ),
+    (
+        4, 5, 7, 6, 20, 21, 22, 32, 11, 37, 36, 23, 9, 8, 33, 10, 38, 30, 40, 42, 34, 15, 31, 41,
+        28, 13, 14, 43, 26, 18, 27, 19, 29, 24, 2, 25, 12, 39, 17, 16, 35, 0, 1, 3,
     ),
 )
 INNER = (
     (
-        3, 2, 1, 1, 0, 0, 1, 3, 1, 0, 2, 1, 24, 2, 1, 0, 3, 1, 0, 1, 1, 1, 1, 1,
-        1, 0, 29, 0, 0, 23, 2, 0, 1, 3, 0, 0, 0, 1, 0, 1, 3, 1, 1, 2, 25, 0, 0, 1,
-        0, 1, 1, 7, 0, 5, 3, 2, 0, 1, 18, 0, 22, 0, 1, 1, 0, 0, 1, 0, 0, 20, 3, 1,
-        1, 0, 1, 1, 6, 2, 1, 0, 0, 1, 3, 0, 0, 0, 13, 0, 4, 0, 0, 2, 1, 28, 10, 8,
-        1, 0, 12, 1, 0, 0, 1, 0, 0, 1, 1, 1, 0, 14, 1, 21, 11, 0, 9, 1, 0, 33, 0, 0,
-        16, 15, 30, 1, 1, 0, 1, 19, 1, 26, 17, 27, 35, 37, 34, 31, 32, 36,
-    ),
-    (
-        3, 2, 0, 0, 3, 0, 1, 0, 1, 2, 0, 0, 0, 3, 0, 25, 0, 2, 0, 0, 0, 0, 1, 1,
-        2, 1, 0, 3, 22, 1, 0, 0, 0, 1, 0, 0, 1, 1, 3, 1, 0, 24, 0, 1, 1, 1, 2, 1,
-        0, 0, 1, 0, 1, 1, 3, 0, 0, 23, 2, 1, 6, 0, 1, 1, 0, 1, 7, 1, 0, 2, 0, 1,
-        1, 1, 0, 3, 2, 0, 0, 0, 1, 3, 1, 0, 1, 0, 1, 1, 1, 1, 0, 10, 1, 0, 1, 0,
-        28, 8, 27, 0, 1, 14, 4, 1, 1, 0, 12, 1, 1, 11, 33, 26, 1, 0, 1, 1, 20, 9, 29, 0,
-        16, 0, 5, 1, 17, 31, 32, 15, 13, 19, 21, 1, 37, 35, 18, 30, 36, 34,
+        2, 3, 1, 1, 0, 0, 1, 1, 0, 3, 2, 1, 2, 29, 1, 0, 3, 1, 0, 1, 1, 1, 1, 1,
+        1, 1, 0, 0, 0, 3, 1, 2, 0, 7, 0, 0, 0, 0, 0, 0, 1, 3, 5, 1, 1, 1, 2, 0,
+        0, 0, 1, 2, 0, 3, 0, 1, 1, 1, 0, 0, 0, 1, 1, 3, 0, 6, 1, 1, 2, 0, 0, 28,
+        0, 1, 3, 0, 0, 0, 1, 0, 0, 1, 2, 1, 1, 0, 0, 1, 1, 8, 16, 1, 1, 10, 1, 1,
+        14, 9, 4, 0, 0, 11, 37, 34, 13, 1, 0, 1, 17, 35, 0, 15, 26, 0, 0, 12, 36, 1, 1, 0,
+        0, 1, 0, 27, 1, 0,
+    ),
+    (
+        0, 0, 0, 1, 0, 3, 1, 2, 2, 0, 3, 0, 0, 3, 0, 0, 2, 0, 0, 0, 0, 1, 1, 1,
+        0, 2, 0, 1, 1, 0, 0, 0, 1, 1, 3, 0, 1, 0, 1, 3, 0, 1, 1, 1, 1, 1, 2, 1,
+        0, 3, 1, 2, 0, 6, 1, 0, 0, 1, 0, 7, 0, 0, 1, 1, 1, 2, 0, 3, 1, 0, 0, 1,
+        2, 3, 1, 1, 0, 1, 0, 1, 0, 0, 0, 0, 10, 0, 0, 1, 1, 1, 0, 1, 0, 1, 29, 27,
+        1, 0, 0, 1, 11, 0, 8, 1, 9, 14, 28, 16, 1, 1, 5, 15, 17, 1, 13, 26, 4, 12, 1, 36,
+        1, 1, 35, 1, 34, 37,
+    ),
+    (
+        1, 1, 0, 0, 1, 2, 1, 0, 2, 1, 3, 2, 1, 0, 3, 3, 1, 0, 1, 1, 1, 1, 1, 1,
+        0, 1, 0, 0, 2, 1, 0, 0, 0, 6, 1, 1, 0, 1, 0, 0, 2, 3, 0, 1, 0, 3, 7, 1,
+        0, 0, 1, 2, 3, 0, 1, 1, 0, 20, 0, 0, 5, 4, 0, 1, 21, 1, 3, 0, 2, 8, 0, 1,
+        18, 0, 10, 1, 1, 1, 3, 0, 0, 1, 0, 2, 13, 1, 0, 14, 1, 1, 0, 9, 1, 0, 0, 19,
+        1, 12, 1, 15, 11, 1, 0, 0, 0, 0, 0, 0, 1, 1, 1, 1, 0, 0, 37, 0, 0, 16, 1, 1,
+        36, 0, 1, 17, 34, 35,
+    ),
+    (
+        2, 0, 3, 0, 0, 1, 0, 1, 2, 0, 0, 0, 3, 3, 0, 0, 2, 0, 0, 0, 0, 1, 1, 0,
+        0, 1, 1, 1, 2, 1, 0, 0, 0, 1, 3, 0, 1, 1, 3, 1, 0, 1, 0, 0, 1, 1, 2, 0,
+        0, 1, 0, 0, 1, 6, 2, 1, 3, 0, 1, 1, 1, 1, 10, 1, 0, 2, 1, 0, 0, 1, 3, 11,
+        0, 2, 0, 1, 3, 0, 0, 1, 0, 1, 1, 1, 7, 0, 1, 0, 0, 8, 1, 1, 0, 0, 0, 1,
+        1, 0, 1, 14, 1, 1, 4, 5, 12, 1, 1, 9, 1, 15, 20, 0, 13, 1, 16, 18, 1, 0, 1, 17,
+        19, 37, 21, 35, 36, 34,
+    ),
+    (
+        1, 1, 0, 0, 1, 3, 3, 1, 2, 0, 2, 1, 2, 1, 0, 3, 1, 0, 1, 1, 1, 1, 0, 1,
+        0, 0, 2, 3, 0, 0, 1, 7, 0, 1, 1, 0, 1, 0, 0, 1, 1, 2, 0, 0, 5, 3, 0, 0,
+        1, 1, 2, 1, 1, 1, 0, 1, 3, 0, 0, 1, 0, 0, 1, 0, 3, 1, 1, 2, 0, 0, 1, 0,
+        1, 3, 0, 0, 1, 4, 0, 35, 0, 2, 0, 0, 1, 1, 8, 0, 1, 1, 0, 0, 1, 0, 10, 0,
+        0, 0, 1, 1, 9, 1, 1, 1, 14, 1, 34, 6, 11, 36, 0, 0, 1, 13, 15, 12, 37, 33, 16, 32,
+        0, 17, 0, 31, 1, 30,
+    ),
+    (
+        0, 0, 0, 1, 0, 2, 1, 2, 0, 0, 3, 0, 3, 3, 0, 0, 2, 0, 0, 0, 0, 1, 1, 0,
+        1, 1, 1, 0, 1, 2, 1, 0, 1, 0, 3, 0, 3, 0, 0, 0, 1, 1, 2, 1, 0, 1, 0, 1,
+        7, 3, 0, 2, 1, 0, 0, 0, 1, 1, 1, 0, 1, 2, 1, 0, 1, 3, 1, 0, 1, 0, 1, 1,
+        33, 2, 3, 1, 0, 0, 1, 6, 1, 0, 1, 0, 1, 0, 1, 0, 1, 10, 1, 0, 0, 12, 1, 1,
+        0, 13, 0, 0, 0, 1, 1, 14, 32, 1, 17, 31, 1, 8, 16, 9, 35, 37, 11, 0, 5, 15, 1, 34,
+        4, 30, 1, 1, 36, 1,
+    ),
+    (
+        1, 2, 3, 1, 0, 0, 1, 3, 1, 0, 2, 1, 2, 1, 0, 3, 1, 0, 1, 1, 0, 1, 1, 1,
+        0, 0, 3, 24, 1, 1, 2, 0, 0, 0, 1, 1, 22, 0, 1, 1, 1, 0, 1, 0, 0, 0, 2, 6,
+        1, 3, 0, 7, 0, 23, 2, 1, 0, 3, 0, 0, 1, 25, 0, 0, 8, 3, 5, 0, 1, 2, 1, 0,
+        1, 1, 0, 1, 1, 0, 13, 4, 3, 1, 0, 9, 0, 1, 0, 2, 1, 10, 0, 0, 1, 0, 14, 1,
+        1, 1, 0, 0, 11, 0, 0, 1, 0, 0, 1, 0, 1, 0, 12, 0, 1, 0, 1, 15, 0, 16, 1, 1,
+        17, 37, 35, 1, 36, 34,
+    ),
+    (
+        2, 3, 0, 0, 0, 1, 0, 1, 2, 0, 3, 0, 0, 3, 0, 0, 2, 0, 0, 0, 0, 1, 0, 0,
+        1, 1, 2, 1, 22, 0, 0, 3, 1, 1, 0, 25, 0, 23, 0, 1, 0, 1, 6, 1, 2, 1, 1, 0,
+        3, 2, 1, 3, 1, 0, 7, 1, 1, 1, 1, 1, 0, 0, 1, 0, 0, 1, 2, 0, 0, 3, 0, 1,
+        10, 1, 1, 14, 0, 12, 2, 3, 0, 0, 0, 0, 1, 0, 0, 0, 1, 0, 1, 11, 1, 1, 8, 1,
+        1, 15, 1, 4, 1, 1, 1, 13, 9, 1, 1, 1, 0, 5, 0, 16, 1, 1, 24, 1, 0, 1, 1, 37,
+        0, 35, 17, 36, 0, 34,
     ),
 )
 OUTER = (
     (
-        1, 8, 4, 0, 0, 1, 9, 0, 22, 10, 5, 18, 19, 6, 12, 0, 28, 23, 14, 1, 20, 7, 1, 24,
-        15, 32, 21, 11, 34, 16, 26, 29, 30, 25, 36, 33, 13, 17, 27, 31, 37, 35,
-    ),
-    (
-        0, 0, 0, 1, 1, 0, 4, 12, 5, 10, 6, 28, 18, 22, 19, 14, 1, 24, 20, 13, 11, 15, 1, 21,
-        23, 32, 7, 33, 29, 8, 16, 26, 9, 25, 17, 27, 30, 36, 34, 31, 37, 35,
+        5, 4, 0, 1, 0, 6, 0, 14, 0, 1, 1, 16, 10, 1, 34, 11, 26, 7, 29, 12, 36, 17, 27, 15,
+        28, 37, 35, 13,
+    ),
+    (
+        4, 10, 5, 1, 0, 0, 14, 1, 0, 12, 6, 1, 35, 15, 28, 13, 0, 16, 26, 1, 36, 11, 29, 37,
+        17, 27, 34, 7,
+    ),
+    (
+        0, 9, 1, 0, 0, 0, 5, 4, 8, 1, 1, 19, 1, 18, 14, 21, 6, 7, 20, 15, 16, 34, 12, 36,
+        13, 35, 17, 37,
+    ),
+    (
+        0, 4, 1, 18, 1, 14, 1, 0, 0, 9, 19, 12, 5, 1, 13, 6, 0, 20, 21, 15, 7, 16, 8, 17,
+        34, 37, 36, 35,
+    ),
+    (
+        8, 9, 0, 1, 0, 0, 0, 5, 1, 10, 4, 1, 6, 14, 1, 34, 11, 32, 16, 30, 7, 15, 33, 37,
+        35, 36, 17, 31,
+    ),
+    (
+        0, 1, 1, 9, 1, 4, 10, 0, 0, 14, 0, 15, 32, 5, 8, 33, 6, 34, 1, 11, 17, 31, 16, 30,
+        7, 35, 36, 37,
+    ),
+    (
+        1, 8, 0, 9, 0, 5, 4, 1, 0, 1, 22, 0, 1, 6, 7, 23, 11, 25, 10, 24, 12, 13, 34, 16,
+        17, 36, 37, 35,
+    ),
+    (
+        0, 0, 1, 1, 1, 4, 9, 22, 0, 6, 5, 1, 0, 16, 10, 36, 13, 12, 8, 7, 24, 11, 23, 35,
+        34, 25, 17, 37,
     ),
 )
 NOTHING = 63
@@ -439,6 +511,9 @@
             for l in padded
         ]
 
+        flat = [word for l in words for word in l]
+        role = 4 * X + 2 * Y + side
+
         def one(i, state):
             word, counts = state
             code = lax.rem(word, 64)
@@ -447,7 +522,7 @@
             return lax.div(word, 64), counts
 
         def five(w, counts):
-            return lax.fori_loop(0, 5, one, (pick2(side, w, words), counts))[1]
+            return lax.fori_loop(0, 5, one, (pick(role * size + w, flat), counts))[1]
 
         lax.fori_loop(0, size, five, (jnp.int32(0),) * 4)
 

time: 129 us -> 127 us (0.984)
  the two profiles are of different devices: /device:TPU:4 before, /device:TPU:5 now
where the time goes in v5:
time: 127 us; the launch traced here: 125 us
  Pallas kernels  123 us (97%)
  local copies, waits for them, and re-layouts  1.32 us (1%)
    pallas_call x1, Pallas kernels, one_kernel(): pl.pallas_call(kernel, out_shape=pltpu.VMEM((width, hw), F32), in_specs=[...  123 us

profile of v5, /device:TPU:5, one launch (start us, length us, event | category | flops | bytes accessed | tf_op | source)
XLA Modules:
  0.0 124.7 jit_solution(4104711120203826753)
XLA Ops:
  0.0 123.4 %shard_map.55 = f32[1024,512]{1,0:T(8,128)S(1)} custom-call(bf16[1536,1024]{1,0:T(8,128)(2,1)} %dens.1, s32[1536]{0:T(1024)} %val_band.1, s32[1536]{0:T(1024)} %cond_band.1, f32[128]{0:T(128)} %val_energy.1, f32[256]{0:T(256)} %cond_energy.1), custom_call_target="tpu_custom_call" | custom-call | tf_op jit(solution)/shard_map/pallas_call | solution.py:661
  123.4 1.3 %copy.7 = f32[1024,512]{1,0:T(8,128)} copy(f32[1024,512]{1,0:T(8,128)S(1)} %shard_map.55) | data formatting | bytes 4194304

commit v6 on v4

--- a/solution.py
+++ b/solution.py
@@ -63,46 +63,118 @@
     (2, 1, 0), (2, 0, 0), (3, 1, 0), (3, 0, 0),
     (1, 0, 1), (1, 2, 0), (1, 3, 0),
 )
-INWARD = ((0, 0), (1, 0), (0, 1), (1, 1), (0, 2), (1, 2), (1, 3), (0, 3))
+INWARD = ((1, 0), (0, 0), (0, 1), (1, 1), (0, 2), (1, 2), (1, 3), (0, 3))
 ARRIVALS = 8
 RING, SENDS = 8, 4
 COUNT = 44
 PIECES = (
     (
-        5, 6, 20, 4, 11, 36, 10, 32, 21, 16, 17, 8, 7, 19, 33, 0, 23, 2, 3, 38, 18, 1, 37, 22,
-        34, 30, 26, 31, 27, 28, 24, 40, 29, 42, 35, 12, 25, 43, 15, 39, 41, 13, 9, 14,
-    ),
-    (
-        20, 7, 4, 6, 22, 32, 21, 5, 10, 33, 9, 36, 23, 38, 30, 11, 37, 40, 41, 15, 14, 31, 8, 42,
-        34, 13, 28, 39, 24, 26, 18, 43, 1, 16, 27, 29, 35, 19, 25, 2, 12, 17, 3, 0,
+        5, 6, 4, 11, 21, 7, 10, 20, 18, 22, 36, 37, 32, 17, 16, 23, 19, 1, 33, 3, 0, 8, 26, 38,
+        30, 27, 34, 31, 2, 9, 24, 28, 39, 25, 43, 35, 29, 42, 40, 41, 14, 15, 13, 12,
+    ),
+    (
+        4, 5, 7, 6, 32, 21, 22, 20, 11, 9, 23, 33, 37, 36, 38, 41, 31, 14, 42, 40, 15, 12, 8, 34,
+        13, 28, 30, 43, 19, 39, 27, 26, 10, 24, 25, 18, 29, 1, 17, 35, 16, 2, 3, 0,
     ),
 )
 INNER = (
     (
-        3, 2, 1, 1, 0, 0, 1, 3, 1, 0, 2, 1, 24, 2, 1, 0, 3, 1, 0, 1, 1, 1, 1, 1,
-        1, 0, 29, 0, 0, 23, 2, 0, 1, 3, 0, 0, 0, 1, 0, 1, 3, 1, 1, 2, 25, 0, 0, 1,
-        0, 1, 1, 7, 0, 5, 3, 2, 0, 1, 18, 0, 22, 0, 1, 1, 0, 0, 1, 0, 0, 20, 3, 1,
-        1, 0, 1, 1, 6, 2, 1, 0, 0, 1, 3, 0, 0, 0, 13, 0, 4, 0, 0, 2, 1, 28, 10, 8,
-        1, 0, 12, 1, 0, 0, 1, 0, 0, 1, 1, 1, 0, 14, 1, 21, 11, 0, 9, 1, 0, 33, 0, 0,
-        16, 15, 30, 1, 1, 0, 1, 19, 1, 26, 17, 27, 35, 37, 34, 31, 32, 36,
-    ),
-    (
-        3, 2, 0, 0, 3, 0, 1, 0, 1, 2, 0, 0, 0, 3, 0, 25, 0, 2, 0, 0, 0, 0, 1, 1,
-        2, 1, 0, 3, 22, 1, 0, 0, 0, 1, 0, 0, 1, 1, 3, 1, 0, 24, 0, 1, 1, 1, 2, 1,
-        0, 0, 1, 0, 1, 1, 3, 0, 0, 23, 2, 1, 6, 0, 1, 1, 0, 1, 7, 1, 0, 2, 0, 1,
-        1, 1, 0, 3, 2, 0, 0, 0, 1, 3, 1, 0, 1, 0, 1, 1, 1, 1, 0, 10, 1, 0, 1, 0,
-        28, 8, 27, 0, 1, 14, 4, 1, 1, 0, 12, 1, 1, 11, 33, 26, 1, 0, 1, 1, 20, 9, 29, 0,
-        16, 0, 5, 1, 17, 31, 32, 15, 13, 19, 21, 1, 37, 35, 18, 30, 36, 34,
+        0, 1, 0, 2, 3, 1, 0, 2, 0, 1, 1, 1, 1, 2, 3, 1, 3, 0, 1, 0, 1, 1, 6, 7,
+        1, 0, 1, 0, 1, 1, 1, 3, 2, 0, 1, 0, 1, 1, 0, 1, 3, 0, 0, 1, 0, 2, 0, 1,
+        1, 2, 0, 3, 1, 0, 0, 0, 1, 0, 0, 0, 1, 28, 0, 1, 3, 0, 1, 0, 2, 0, 0, 1,
+        1, 1, 3, 0, 0, 0, 1, 35, 0, 5, 2, 1, 1, 0, 1, 0, 1, 4, 1, 8, 0, 10, 1, 1,
+        0, 1, 0, 12, 1, 1, 14, 9, 11, 15, 1, 0, 0, 13, 0, 1, 16, 27, 36, 34, 0, 0, 0, 37,
+        29, 0, 0, 17, 1, 26,
+    ),
+    (
+        3, 1, 2, 0, 0, 1, 0, 1, 2, 0, 1, 0, 3, 0, 0, 0, 3, 2, 0, 1, 0, 0, 0, 2,
+        0, 0, 1, 3, 0, 0, 0, 0, 0, 1, 0, 1, 0, 1, 7, 6, 1, 0, 3, 1, 2, 1, 0, 0,
+        1, 1, 1, 2, 1, 0, 1, 3, 1, 0, 1, 0, 1, 0, 1, 0, 2, 0, 1, 0, 1, 1, 1, 0,
+        3, 1, 1, 29, 3, 0, 2, 0, 1, 0, 1, 1, 0, 0, 0, 0, 0, 1, 1, 0, 27, 1, 10, 26,
+        0, 1, 1, 1, 0, 8, 17, 14, 1, 0, 11, 9, 28, 1, 16, 1, 15, 1, 5, 1, 4, 13, 1, 12,
+        1, 37, 36, 35, 1, 34,
+    ),
+    (
+        0, 1, 0, 2, 1, 0, 2, 3, 0, 1, 1, 1, 1, 2, 1, 3, 0, 3, 1, 0, 1, 0, 3, 0,
+        1, 2, 0, 1, 1, 0, 0, 6, 1, 4, 0, 1, 1, 0, 1, 0, 3, 1, 1, 1, 0, 1, 2, 1,
+        2, 3, 7, 1, 1, 19, 0, 0, 21, 0, 0, 0, 0, 1, 1, 0, 3, 0, 18, 1, 1, 2, 0, 1,
+        1, 0, 0, 1, 1, 0, 3, 0, 0, 5, 8, 12, 9, 0, 1, 13, 0, 0, 1, 2, 20, 14, 11, 10,
+        1, 1, 0, 1, 15, 1, 0, 0, 0, 0, 0, 1, 0, 0, 1, 0, 0, 36, 1, 0, 16, 1, 0, 35,
+        1, 1, 1, 37, 17, 34,
+    ),
+    (
+        1, 0, 0, 2, 1, 0, 2, 1, 0, 1, 3, 0, 3, 0, 0, 0, 3, 2, 0, 1, 0, 1, 0, 2,
+        0, 1, 1, 0, 1, 0, 0, 1, 0, 3, 0, 2, 1, 0, 3, 0, 0, 0, 1, 0, 0, 0, 6, 2,
+        0, 3, 0, 1, 0, 1, 1, 0, 7, 1, 1, 1, 0, 0, 1, 1, 1, 2, 1, 3, 0, 1, 1, 11,
+        2, 0, 1, 3, 1, 0, 0, 1, 1, 1, 0, 0, 1, 0, 10, 0, 1, 1, 1, 0, 1, 1, 0, 1,
+        9, 0, 5, 1, 8, 15, 1, 14, 1, 1, 1, 13, 19, 1, 0, 35, 0, 16, 0, 4, 1, 12, 20, 1,
+        17, 34, 21, 37, 18, 36,
+    ),
+    (
+        0, 2, 1, 0, 3, 1, 0, 0, 2, 1, 1, 1, 1, 2, 3, 1, 3, 0, 1, 0, 1, 1, 3, 2,
+        0, 0, 1, 0, 0, 1, 0, 0, 0, 1, 1, 1, 1, 7, 1, 3, 1, 1, 0, 1, 1, 1, 2, 2,
+        1, 0, 0, 0, 0, 1, 1, 3, 0, 0, 4, 0, 1, 3, 0, 0, 1, 0, 0, 2, 1, 0, 34, 5,
+        1, 0, 3, 0, 0, 0, 6, 1, 0, 0, 0, 2, 1, 0, 0, 8, 0, 0, 1, 1, 0, 1, 1, 35,
+        10, 1, 0, 9, 13, 0, 1, 1, 0, 14, 0, 0, 1, 1, 0, 11, 15, 37, 12, 1, 1, 32, 16, 1,
+        33, 36, 17, 31, 1, 30,
+    ),
+    (
+        1, 0, 3, 2, 0, 1, 0, 1, 2, 0, 1, 0, 3, 0, 0, 0, 3, 2, 0, 1, 0, 0, 0, 34,
+        0, 3, 2, 1, 1, 1, 0, 0, 0, 1, 0, 1, 0, 2, 0, 0, 0, 1, 0, 3, 0, 0, 1, 0,
+        1, 2, 1, 3, 0, 0, 1, 1, 7, 1, 0, 1, 0, 1, 1, 1, 2, 32, 1, 1, 3, 1, 1, 0,
+        0, 1, 0, 3, 0, 2, 0, 1, 1, 0, 0, 1, 0, 13, 1, 1, 1, 1, 0, 35, 1, 0, 6, 12,
+        0, 1, 0, 1, 1, 37, 0, 31, 30, 17, 8, 1, 10, 33, 1, 16, 14, 0, 9, 1, 11, 5, 0, 1,
+        4, 1, 1, 1, 15, 36,
+    ),
+    (
+        3, 0, 1, 0, 1, 2, 0, 0, 2, 1, 1, 1, 1, 2, 3, 1, 23, 3, 0, 1, 0, 0, 1, 1,
+        3, 2, 0, 4, 0, 1, 1, 1, 0, 0, 0, 1, 1, 1, 1, 0, 1, 0, 25, 3, 0, 2, 22, 1,
+        1, 1, 3, 2, 0, 0, 1, 24, 1, 0, 0, 0, 0, 1, 0, 1, 0, 6, 3, 8, 1, 7, 0, 1,
+        5, 1, 1, 0, 1, 2, 1, 0, 1, 3, 0, 0, 12, 9, 0, 0, 0, 1, 0, 2, 13, 0, 1, 0,
+        1, 0, 0, 0, 1, 1, 0, 0, 1, 0, 1, 0, 0, 10, 11, 1, 15, 14, 0, 0, 1, 16, 1, 17,
+        1, 1, 37, 35, 36, 34,
+    ),
+    (
+        2, 3, 1, 0, 0, 1, 2, 0, 1, 0, 1, 0, 0, 0, 3, 22, 0, 3, 2, 0, 1, 0, 1, 0,
+        0, 0, 0, 3, 24, 0, 1, 1, 25, 2, 0, 0, 1, 0, 1, 3, 0, 1, 0, 0, 1, 2, 1, 1,
+        0, 0, 0, 1, 2, 1, 1, 0, 3, 0, 0, 1, 0, 1, 2, 0, 1, 1, 0, 0, 0, 23, 1, 3,
+        6, 1, 7, 1, 1, 3, 0, 2, 0, 1, 0, 1, 1, 0, 1, 1, 1, 1, 0, 1, 0, 1, 0, 11,
+        5, 1, 13, 1, 9, 10, 0, 14, 1, 8, 1, 0, 1, 1, 0, 1, 1, 0, 15, 4, 36, 12, 17, 1,
+        1, 16, 34, 35, 37, 0,
     ),
 )
 OUTER = (
     (
-        1, 8, 4, 0, 0, 1, 9, 0, 22, 10, 5, 18, 19, 6, 12, 0, 28, 23, 14, 1, 20, 7, 1, 24,
-        15, 32, 21, 11, 34, 16, 26, 29, 30, 25, 36, 33, 13, 17, 27, 31, 37, 35,
-    ),
-    (
-        0, 0, 0, 1, 1, 0, 4, 12, 5, 10, 6, 28, 18, 22, 19, 14, 1, 24, 20, 13, 11, 15, 1, 21,
-        23, 32, 7, 33, 29, 8, 16, 26, 9, 25, 17, 27, 30, 36, 34, 31, 37, 35,
+        0, 1, 0, 6, 1, 10, 0, 1, 1, 34, 4, 15, 7, 5, 28, 11, 14, 12, 35, 13, 29, 36, 37, 0,
+        16, 26, 17, 27,
+    ),
+    (
+        10, 1, 0, 13, 0, 5, 1, 14, 0, 12, 0, 4, 11, 15, 28, 29, 34, 17, 27, 1, 6, 36, 35, 16,
+        26, 1, 37, 7,
+    ),
+    (
+        0, 5, 1, 0, 18, 9, 0, 1, 0, 4, 6, 1, 20, 8, 7, 19, 1, 15, 21, 14, 12, 16, 36, 13,
+        17, 34, 37, 35,
+    ),
+    (
+        0, 1, 0, 9, 0, 1, 4, 5, 8, 1, 19, 0, 14, 1, 13, 20, 6, 12, 15, 18, 21, 7, 17, 37,
+        35, 16, 36, 34,
+    ),
+    (
+        4, 1, 1, 0, 0, 5, 9, 10, 6, 0, 1, 1, 0, 7, 11, 15, 8, 33, 36, 37, 14, 34, 32, 35,
+        16, 30, 17, 31,
+    ),
+    (
+        4, 0, 0, 9, 0, 1, 8, 5, 1, 0, 10, 6, 14, 15, 11, 1, 32, 35, 33, 17, 31, 1, 34, 16,
+        30, 36, 7, 37,
+    ),
+    (
+        1, 8, 0, 0, 4, 1, 1, 0, 0, 1, 5, 10, 23, 7, 6, 22, 24, 25, 16, 36, 11, 9, 13, 12,
+        17, 37, 34, 35,
+    ),
+    (
+        0, 0, 4, 1, 0, 5, 1, 0, 1, 23, 12, 22, 9, 10, 6, 1, 13, 17, 11, 8, 35, 7, 37, 24,
+        16, 36, 34, 25,
     ),
 )
 NOTHING = 63
@@ -439,6 +511,9 @@
             for l in padded
         ]
 
+        flat = [word for l in words for word in l]
+        role = 4 * X + 2 * Y + side
+
         def one(i, state):
             word, counts = state
             code = lax.rem(word, 64)
@@ -447,7 +522,7 @@
             return lax.div(word, 64), counts
 
         def five(w, counts):
-            return lax.fori_loop(0, 5, one, (pick2(side, w, words), counts))[1]
+            return lax.fori_loop(0, 5, one, (pick(role * size + w, flat), counts))[1]
 
         lax.fori_loop(0, size, five, (jnp.int32(0),) * 4)
 

time: 129 us -> 125 us (0.969)
  the two profiles are of different devices: /device:TPU:4 before, /device:TPU:5 now
where the time goes in v6:
time: 125 us; the launch traced here: 124 us
  Pallas kernels  122 us (98%)
  local copies, waits for them, and re-layouts  1.32 us (1%)
    pallas_call x1, Pallas kernels, one_kernel(): pl.pallas_call(kernel, out_shape=pltpu.VMEM((width, hw), F32), in_specs=[...  122 us

profile of v6, /device:TPU:5, one launch (start us, length us, event | category | flops | bytes accessed | tf_op | source)
XLA Modules:
  0.0 123.5 jit_solution(10741616191973740709)
XLA Ops:
  0.0 122.2 %shard_map.55 = f32[1024,512]{1,0:T(8,128)S(1)} custom-call(bf16[1536,1024]{1,0:T(8,128)(2,1)} %dens.1, s32[1536]{0:T(1024)} %val_band.1, s32[1536]{0:T(1024)} %cond_band.1, f32[128]{0:T(128)} %val_energy.1, f32[256]{0:T(256)} %cond_energy.1), custom_call_target="tpu_custom_call" | custom-call | tf_op jit(solution)/shard_map/pallas_call | solution.py:661
  122.2 1.3 %copy.7 = f32[1024,512]{1,0:T(8,128)} copy(f32[1024,512]{1,0:T(8,128)S(1)} %shard_map.55) | data formatting | bytes 4194304
